TPU v7x, 32 devices: a whole 2x2x4 slice. The times are simulated.
32 devices in a mesh: scan: 8 (over z, y), grp: 4 (over x, core).
Axes of the slice: x: 2, y: 2, z: 4, core: 2. Of those that a mesh axis runs over, the one named last changes fastest.
Arguments:
- samples: float32 [128, 64, 6, 128], P('scan', 'grp'), may hold values from -6 to 6
- point_count: int32 [128], P('scan'), may hold values from 4096 to 8192
- corr_scan: int32 [128, 64], P('scan', 'grp'), may hold values from 0 to 127, as said below
- corr_tile: int32 [128, 64], P('scan', 'grp'), may hold values from 0 to 63
- corr_src: int32 [128, 64, 128], P('scan', 'grp'), may hold values from 0 to 2047
Outputs:
- hessian: float32 [128, 6, 6, 128], P('scan', None, None, 'grp')
- gradient: float32 [128, 6], P(('scan', 'grp'))
Inputs may be any that keep to these rules, and one draw needn't show every extreme that they name: Never the scan of the entry's own row. A named tile is held by the device with scan index corr_scan // 16 and grp index corr_tile // 16; the 256 entries of one device name at most 16 tiles held by any one device, and in every draw some device is named exactly 16 times by every device.
All inputs are finite; a program needn't handle non-finite values.
Results may differ from a plain program's by a relative error of at most 0.00021.
Values sent between devices are 32-bit elements; how exact they have to be, the bound alone decides.
A program may use at most 64 MiB of HBM per device.

v0:
```python
import functools

import jax
import jax.numpy as jnp
from jax import lax
from jax.experimental import pallas as pl
from jax.experimental.pallas import tpu as pltpu
from jax.sharding import PartitionSpec as P

LANES = 128
VALUES = 32
LEAST_POINTS = 4096
PAIRS = [(i, j) for i in range(6) for j in range(i, 6)]
VMEM = pl.BlockSpec(memory_space=pltpu.VMEM)
SMEM = pl.BlockSpec(memory_space=pltpu.SMEM)


def halves(value, size):
    if size & (size - 1):
        return value // size, value % size
    return value >> (size.bit_length() - 1), value & (size - 1)


def lane_take(table, index):
    return jnp.take_along_axis(table, index, axis=1, mode="promise_in_bounds")


def pack_kernel(cap, n_grp, samples, count, corr_scan, corr_tile, corr_src, data, meta, used):
    scan_local, tiles_local = samples.shape[0], samples.shape[2]
    per_scan = corr_src.shape[1]
    devices = meta.shape[0]
    scan_index, group_index = lax.axis_index("scan"), lax.axis_index("grp")
    first_point = group_index * tiles_local * LANES

    def clear(d, _):
        used[d] = 0
        for j in range(cap):
            meta[d, 0, j] = -1
            meta[d, 0, cap + j] = 0
            meta[d, 0, 2 * cap + j] = -1
        data[pl.ds(pl.multiple_of(d * cap * 4, 8), cap * 4), :] = jnp.zeros((cap * 4, LANES), jnp.float32)
        return 0

    lax.fori_loop(0, devices, clear, 0)

    def one_scan(s, _):
        wanted = corr_src[s]
        tile, lane = wanted >> 7, wanted & (LANES - 1)
        picked = [jnp.zeros((per_scan, LANES), jnp.float32)] * 3
        for t in range(tiles_local):
            hit = tile == t
            for c in range(3):
                row = jnp.broadcast_to(samples[s, c, pl.ds(t, 1), :], (per_scan, LANES))
                picked[c] = jnp.where(hit, lane_take(row, lane), picked[c])
        mask = jnp.where(first_point + wanted < count[s], 1.0, 0.0).astype(jnp.float32)
        picked.append(mask)
        for k in range(per_scan):
            b, t = corr_scan[s, k], corr_tile[s, k]
            (b_dev, b_loc), (t_dev, t_loc) = halves(b, scan_local), halves(t, tiles_local)
            d = b_dev * n_grp + t_dev
            j = used[d]
            used[d] = j + 1
            meta[d, 0, j] = b_loc
            meta[d, 0, cap + j] = t_loc
            meta[d, 0, 2 * cap + j] = scan_index * scan_local + s
            base = d * cap * 4 + j
            for c in range(4):
                data[pl.ds(base + c * cap, 1), :] = picked[c][k : k + 1, :]
        return 0

    lax.fori_loop(0, scan_local, one_scan, 0)


def meet_all(n_grp, devices, me):
    barrier = pltpu.get_barrier_semaphore()

    def hello(k, _):
        peer = lax.rem(me + k, devices)
        pl.semaphore_signal(
            barrier, inc=1, device_id=(peer // n_grp, peer % n_grp), device_id_type=pl.DeviceIdType.MESH
        )
        return 0

    lax.fori_loop(1, devices, hello, 0)
    pl.semaphore_wait(barrier, devices - 1)


def remote(src, dst, send, recv, peer, n_grp):
    return pltpu.make_async_remote_copy(
        src_ref=src, dst_ref=dst, send_sem=send, recv_sem=recv,
        device_id=(peer // n_grp, peer % n_grp), device_id_type=pl.DeviceIdType.MESH,
    )


def exchange_kernel(
    cap, n_grp, samples, count, data, meta, by_source, by_partner,
    data_in, meta_in, codes, comps, sums, packed,
    send_data, recv_data, send_meta, recv_meta, send_src, recv_src, send_part, recv_part, own,
):
    scan_local, tiles_local = samples.shape[0], samples.shape[2]
    n_scan, packed_rows = packed.shape[0], packed.shape[1]
    devices = n_scan * n_grp
    rows = cap * 4
    width = n_grp * cap
    groups = LANES // width
    batch = 16
    scan_index, group_index = lax.axis_index("scan"), lax.axis_index("grp")
    me = scan_index * n_grp + group_index
    lane = lax.broadcasted_iota(jnp.int32, (batch, LANES), 1)
    packed_lane = lax.broadcasted_iota(jnp.int32, (packed_rows, LANES), 1) // width

    full_groups = min(LEAST_POINTS // (tiles_local * LANES), n_grp) if 3 * cap % 8 == 0 else 0
    short = rows - cap

    def send_one(src, dst_index, send_index, recv_index, peer, size):
        return remote(
            data.at[pl.ds(pl.multiple_of(src * rows, 8), size)],
            data_in.at[pl.ds(pl.multiple_of(dst_index * rows, 8), size)],
            send_data.at[send_index], recv_data.at[recv_index], peer, n_grp,
        )

    def send_code(src, dst_index, send_index, recv_index, peer):
        return remote(
            meta.at[src], meta_in.at[dst_index], send_meta.at[send_index], recv_meta.at[recv_index], peer, n_grp
        )

    def to_source(row, holder, peer, recv_index):
        return remote(packed.at[row], by_source.at[holder], send_src.at[peer], recv_src.at[recv_index], peer, n_grp)

    def to_partner(row, at, g):
        peer = scan_index * n_grp + g
        return remote(
            packed.at[row], by_partner.at[at, row], send_part.at[g, row], recv_part.at[at, row], peer, n_grp
        )

    meet_all(n_grp, devices, me)

    def start_meta(k, _):
        peer = lax.rem(me + k, devices)
        send_code(peer, me, peer, me, peer).start()
        return 0

    def start_data(k, _):
        peer = lax.rem(me + k, devices)

        @pl.when(group_index < full_groups)
        def _():
            send_one(peer, me, peer, me, peer, short).start()

        @pl.when(group_index >= full_groups)
        def _():
            send_one(peer, me, peer, me, peer, rows).start()

        return 0

    def wait_meta(k, _):
        peer = lax.rem(me + k, devices)
        copy = send_code(peer, peer, peer, peer, peer)
        copy.wait_send()
        copy.wait_recv()
        return 0

    lax.fori_loop(1, devices, start_meta, 0)
    lax.fori_loop(1, devices, start_data, 0)
    own_data = pltpu.make_async_copy(
        data.at[pl.ds(pl.multiple_of(me * rows, 8), rows)], data_in.at[pl.ds(pl.multiple_of(me * rows, 8), rows)], own.at[0]
    )
    own_meta = pltpu.make_async_copy(meta.at[me], meta_in.at[me], own.at[1])
    own_data.start()
    own_meta.start()
    sums[...] = jnp.zeros_like(sums)
    own_data.wait()
    own_meta.wait()

    def no_mask(row, _):
        for g in range(full_groups):
            first = pl.multiple_of((row * n_grp + g) * rows + short, 8)
            data_in[pl.ds(first, cap), :] = jnp.ones((cap, LANES), jnp.float32)
        return 0

    lax.fori_loop(0, n_scan, no_mask, 0)
    lax.fori_loop(1, devices, wait_meta, 0)
    to_scalar = pltpu.make_async_copy(meta_in, codes, own.at[2])
    to_scalar.start()
    to_scalar.wait()

    def one_batch(i, row):
        for j in range(batch):
            step, place = halves(i * batch + j, cap)
            d = row * n_grp + step
            b, t = codes[d, 0, place], codes[d, 0, cap + place]
            source = codes[d, 0, 2 * cap + place]
            safe = jnp.maximum(b, 0)
            limit = count[safe] - (group_index * tiles_local + t) * LANES
            partner = jnp.where(b < 0, -1, scan_index * scan_local + b)
            for c in range(6):
                comps[c, j : j + 1, :] = samples[safe, c, pl.ds(t, 1), :]
            comps[6, j : j + 1, :] = jnp.full((1, LANES), limit.astype(jnp.float32))
            comps[7, j : j + 1, :] = jnp.full((1, LANES), partner.astype(jnp.float32))
            comps[8, j : j + 1, :] = jnp.full((1, LANES), source.astype(jnp.float32))
        count_in = max(batch // cap, 1)
        read = []
        for c in range(4):
            pieces = []
            for piece in range(count_in):
                step, place = halves(i * batch + piece * cap, cap)
                base = (row * n_grp + step) * rows + c * cap + place
                pieces.append(data_in[pl.ds(base, min(batch, cap)), :])
            read.append(pieces[0] if count_in == 1 else jnp.concatenate(pieces, axis=0))
        px, py, pz, mask = read
        valid = lane < comps[6].astype(jnp.int32)
        nx, ny, nz = [jnp.where(valid, comps[c], 0.0) for c in (3, 4, 5)]
        residual = nx * (px - comps[0]) + ny * (py - comps[1]) + nz * (pz - comps[2])
        weight = mask / (1.0 + residual * residual)
        jac = [py * nz - pz * ny, pz * nx - px * nz, px * ny - py * nx, nx, ny, nz]
        scaled = [weight * x for x in jac]
        products = [scaled[a] * jac[b] for a, b in PAIRS] + [x * residual for x in scaled]
        total = jnp.zeros((batch, LANES), jnp.float32)
        for q, product in enumerate(products):
            total = jnp.where(lane == q, jnp.sum(product, axis=1, keepdims=True), total)
        total = jnp.where(lane == 27, comps[8], total)
        total = jnp.where(lane == 28, comps[7], total)
        sums[pl.ds(pl.multiple_of(i * batch, batch), batch), :] = total
        return row

    def one_row(k, _):
        row = lax.rem(scan_index + n_scan - k, n_scan)
        for g in range(n_grp):
            source = row * n_grp + g

            @pl.when(source != me)
            def _():
                send_one(source, source, source, source, source, short if g < full_groups else rows).wait_recv()

        lax.fori_loop(0, width // batch, one_batch, row)
        turned = sums[...].T
        result = turned[0:packed_rows, :]
        for g in range(1, groups):
            moved = pltpu.roll(turned[g * packed_rows : (g + 1) * packed_rows, :], g * width, 1)
            result = jnp.where(packed_lane == g, moved, result)
        packed[row] = result
        by_partner[group_index, row] = result
        for g in range(n_grp):
            peer = row * n_grp + g

            @pl.when(peer != me)
            def _():
                to_source(row, me, peer, me).start()

        @pl.when(row == scan_index)
        def _():
            by_source[me] = result

        for g in range(1, n_grp):
            to_partner(row, group_index, lax.rem(group_index + g, n_grp)).start()
        return 0

    lax.fori_loop(0, n_scan, one_row, 0)

    def finish(k, _):
        peer = lax.rem(me + k, devices)

        @pl.when(group_index < full_groups)
        def _():
            send_one(peer, peer, peer, peer, peer, short).wait_send()

        @pl.when(group_index >= full_groups)
        def _():
            send_one(peer, peer, peer, peer, peer, rows).wait_send()

        copy = to_source(0, peer, peer, peer)
        copy.wait_send()
        copy.wait_recv()
        return 0

    lax.fori_loop(1, devices, finish, 0)

    def finish_partner(row, _):
        for k in range(1, n_grp):
            g = lax.rem(group_index + k, n_grp)
            copy = to_partner(row, g, g)
            copy.wait_send()
            copy.wait_recv()
        return 0

    lax.fori_loop(0, n_scan, finish_partner, 0)


def regroup(parts, width):
    groups = len(parts)
    lane = lax.broadcasted_iota(jnp.int32, parts[0].shape, 1) // width
    out = []
    for b in range(groups):
        total = parts[b]
        for g in range(groups):
            if g != b:
                total = jnp.where(lane == g, pltpu.roll(parts[g], (g - b) * width % LANES, 1), total)
        out.append(total)
    return out


def assemble_kernel(n_grp, width, by_source, by_partner, hessian, gradient, total):
    rows, columns = hessian.shape[2], hessian.shape[3]
    grad_rows = gradient.shape[0]
    packed_rows = by_source.shape[1]
    groups = LANES // width
    scan_index, group_index = lax.axis_index("scan"), lax.axis_index("grp")
    cells = rows * columns
    total[...] = jnp.zeros_like(total)
    step = 2 * groups

    def place(ids, first, size):
        local = ids - first
        return local, (local >= 0) & (local < size)

    def add(read, sign):
        def body(i, _):
            turned = []
            for half in range(2):
                parts = [read(i * step + half * groups + g) for g in range(groups)]
                turned.append(jnp.concatenate(regroup(parts, width), axis=0))
            values = jnp.concatenate(turned, axis=1)
            source, partner = values[27:28, :].astype(jnp.int32), values[28:29, :].astype(jnp.int32)
            own, other = (source, partner) if sign > 0 else (partner, source)
            row, row_ok = place(own, scan_index * rows, rows)
            plus, plus_ok = place(own, group_index * columns, columns)
            minus, minus_ok = place(other, group_index * columns, columns)
            plus = jnp.where(row_ok & plus_ok, row * columns + plus, -1)
            minus = jnp.where(row_ok & minus_ok, row * columns + minus, -1)
            grad, grad_ok = place(row, group_index * grad_rows, grad_rows)
            grad = jnp.where(row_ok & grad_ok, grad, -1)
            cell = lax.broadcasted_iota(jnp.int32, (cells, 2 * LANES), 0)
            chosen = jnp.where(cell == plus, 1.0, jnp.where(cell == minus, -1.0, 0.0))
            short = lax.broadcasted_iota(jnp.int32, (16, 2 * LANES), 0)
            chosen_grad = jnp.where(short == grad, float(sign), 0.0)
            matrix = jnp.concatenate([chosen, chosen_grad], axis=0).astype(jnp.bfloat16)
            high = values.astype(jnp.bfloat16)
            low = (values - high.astype(jnp.float32)).astype(jnp.bfloat16)
            both = jnp.concatenate([high, low], axis=0)
            total[...] += lax.dot_general(
                matrix, both, (((1,), (1,)), ((), ())), preferred_element_type=jnp.float32
            )
            return 0

        return body

    blocks = by_source.shape[0]
    n_scan = by_partner.shape[1]
    lax.fori_loop(0, blocks // step, add(lambda k: by_source[k], 1), 0)
    lax.fori_loop(0, blocks // step, add(lambda k: by_partner[k // n_scan, k % n_scan], -1), 0)
    result = total[:, 0:VALUES] + total[:, VALUES : 2 * VALUES]
    turned = result[0:cells, :].T
    where = {pair: q for q, pair in enumerate(PAIRS)}
    for i in range(6):
        ids = [where[min(i, j), max(i, j)] for j in range(6)]
        band = jnp.concatenate([turned[q : q + 1, :] for q in ids], axis=0)
        for r in range(rows):
            hessian[i, :, r, :] = band[:, r * columns : (r + 1) * columns]
    gradient[...] = result[cells : cells + grad_rows, 21:27]


def local(samples, point_count, corr_scan, corr_tile, corr_src):
    f32, i32 = jnp.float32, jnp.int32
    scan_local = samples.shape[0]
    request_count = scan_local * corr_scan.shape[1]
    n_scan, n_grp = lax.axis_size("scan"), lax.axis_size("grp")
    devices = n_scan * n_grp
    cap = 2 * request_count // devices
    width = n_grp * cap
    packed_rows = VALUES * width // LANES
    columns = scan_local * n_scan // n_grp
    grad_rows = scan_local // n_grp
    shape = jax.ShapeDtypeStruct
    dma = pltpu.SemaphoreType.DMA

    tiles = samples.transpose(0, 2, 1, 3)
    data, meta = pl.pallas_call(
        functools.partial(pack_kernel, cap, n_grp),
        out_shape=(shape((devices * cap * 4, LANES), f32), shape((devices, 1, LANES), i32)),
        in_specs=[VMEM, SMEM, SMEM, SMEM, VMEM],
        out_specs=(VMEM, SMEM),
        scratch_shapes=[pltpu.SMEM((devices,), i32)],
    )(tiles, point_count, corr_scan, corr_tile, corr_src)

    by_source, by_partner = pl.pallas_call(
        functools.partial(exchange_kernel, cap, n_grp),
        out_shape=(
            shape((devices, packed_rows, LANES), f32),
            shape((n_grp, n_scan, packed_rows, LANES), f32),
        ),
        in_specs=[VMEM, SMEM, VMEM, VMEM],
        out_specs=(VMEM, VMEM),
        scratch_shapes=[
            pltpu.VMEM(data.shape, f32),
            pltpu.VMEM(meta.shape, i32),
            pltpu.SMEM(meta.shape, i32),
            pltpu.VMEM((9, 16, LANES), f32),
            pltpu.VMEM((LANES, LANES), f32),
            pltpu.VMEM((n_scan, packed_rows, LANES), f32),
        ]
        + [dma((devices,))] * 6
        + [dma((n_grp, n_scan))] * 2
        + [dma((3,))],
        compiler_params=pltpu.CompilerParams(collective_id=0, has_side_effects=True),
    )(tiles, point_count, data, meta)

    hessian, gradient = pl.pallas_call(
        functools.partial(assemble_kernel, n_grp, width),
        out_shape=(shape((6, 6, scan_local, columns), f32), shape((grad_rows, 6), f32)),
        in_specs=[VMEM, VMEM],
        out_specs=(VMEM, VMEM),
        scratch_shapes=[pltpu.VMEM((scan_local * columns + 16, 2 * VALUES), f32)],
    )(by_source, by_partner)
    return hessian.transpose(2, 0, 1, 3), gradient


def solution(mesh):
    placed = (
        P("scan", "grp", None, None),
        P("scan"),
        P("scan", "grp"),
        P("scan", "grp"),
        P("scan", "grp", None),
    )
    return jax.shard_map(
        local,
        mesh=mesh,
        in_specs=placed,
        out_specs=(P("scan", None, None, "grp"), P(("scan", "grp"), None)),
        check_vma=False,
    )
```

profile of v0, /device:TPU:0, one launch (start us, length us, event | category | flops | bytes accessed | tf_op | source)
XLA Modules:
  0.0 63.7 jit_solution(13091038301344580034)
XLA Ops:
  0.6 6.7 %shard_map.68 = (f32[2048,128]{1,0:T(8,128)}, s32[32,1,128]{2,1,0:T(1,128)}) custom-call(f32[16,6,16,128]{3,2,1,0:T(8,128)} %bitcast.2, s32[16]{0:T(128)} %count.3, s32[16,16]{1,0:T(8,128)} %corr_scan.1, s32[16,16]{1,0:T(8,128)} %corr_tile.1, s32[16,16,128]{2,1,0:T(8,128)} %corr_src.1), custom_call_target="tpu_custom_call" | custom-call | tf_op jit(solution)/shard_map/pallas_call | solution.py:377
  7.4 48.6 %shard_map.69 = (f32[32,16,128]{2,1,0:T(8,128)}, f32[4,8,16,128]{3,2,1,0:T(8,128)}) custom-call(f32[16,6,16,128]{3,2,1,0:T(8,128)} %bitcast.3, s32[16]{0:T(128)} %count.3, f32[2048,128]{1,0:T(8,128)} %get-tuple-element.8.data, s32[32,1,128]{2,1,0:T(1,128)} %get-tuple-element.9.meta), custom_call_target="tpu_custom_call" | custom-call | tf_op jit(solution)/shard_map/pallas_call | solution.py:385
  56.0 7.7 %shard_map.70 = (f32[6,6,16,32]{3,2,1,0:T(8,128)}, f32[4,6]{1,0:T(4,128)}) custom-call(f32[32,16,128]{2,1,0:T(8,128)} %get-tuple-element.10.by_source, f32[4,8,16,128]{3,2,1,0:T(8,128)} %get-tuple-element.11.by_partner), custom_call_target="tpu_custom_call" | custom-call | tf_op jit(solution)/shard_map/pallas_call | solution.py:407
where the time goes:
time: 63.8 us; the launch traced here: 63.7 us
  Pallas kernels  63 us (99%)
  between operations  0.65 us (1%)
    pallas_call x1, Pallas kernels, local(): pl.pallas_call(functools.partial(exchange_kernel, cap, n_grp), out_shape=...  48.6 us
    pallas_call x1, Pallas kernels, local(): pl.pallas_call(functools.partial(assemble_kernel, n_grp, width), out_shap...  7.69 us
    pallas_call x1, Pallas kernels, local(): pl.pallas_call(functools.partial(pack_kernel, cap, n_grp), out_shape=(sha...  6.73 us

commit v1 on v0

v1 whole, which is shorter than its diff:
```python
import functools

import jax
import jax.numpy as jnp
from jax import lax
from jax.experimental import pallas as pl
from jax.experimental.pallas import tpu as pltpu
from jax.sharding import PartitionSpec as P

LANES = 128
VALUES = 32
LEAST_POINTS = 4096
PAIRS = [(i, j) for i in range(6) for j in range(i, 6)]
VMEM = pl.BlockSpec(memory_space=pltpu.VMEM)
SMEM = pl.BlockSpec(memory_space=pltpu.SMEM)


def halves(value, size):
    if size & (size - 1):
        return value // size, value % size
    return value >> (size.bit_length() - 1), value & (size - 1)


def lane_take(table, index):
    return jnp.take_along_axis(table, index, axis=1, mode="promise_in_bounds")


def pack_kernel(cap, n_grp, samples, count, corr_scan, corr_tile, corr_src, data, meta, used):
    scan_local, tiles_local = samples.shape[0], samples.shape[2]
    per_scan = corr_src.shape[1]
    devices = meta.shape[0]
    scan_index, group_index = lax.axis_index("scan"), lax.axis_index("grp")
    first_point = group_index * tiles_local * LANES

    def clear(d, _):
        used[d] = 0
        for j in range(cap):
            meta[d, 0, j] = -1
            meta[d, 0, cap + j] = 0
            meta[d, 0, 2 * cap + j] = -1
        data[pl.ds(pl.multiple_of(d * cap * 4, 8), cap * 4), :] = jnp.zeros((cap * 4, LANES), jnp.float32)
        return 0

    lax.fori_loop(0, devices, clear, 0)

    def one_scan(s, _):
        wanted = corr_src[s]
        tile, lane = wanted >> 7, wanted & (LANES - 1)
        picked = [jnp.zeros((per_scan, LANES), jnp.float32)] * 3
        for t in range(tiles_local):
            hit = tile == t
            for c in range(3):
                row = jnp.broadcast_to(samples[s, c, pl.ds(t, 1), :], (per_scan, LANES))
                picked[c] = jnp.where(hit, lane_take(row, lane), picked[c])
        mask = jnp.where(first_point + wanted < count[s], 1.0, 0.0).astype(jnp.float32)
        picked.append(mask)
        for k in range(per_scan):
            b, t = corr_scan[s, k], corr_tile[s, k]
            (b_dev, b_loc), (t_dev, t_loc) = halves(b, scan_local), halves(t, tiles_local)
            d = b_dev * n_grp + t_dev
            j = used[d]
            used[d] = j + 1
            meta[d, 0, j] = b_loc
            meta[d, 0, cap + j] = b_loc * tiles_local + t_loc
            meta[d, 0, 2 * cap + j] = scan_index * scan_local + s
            base = d * cap * 4 + j
            for c in range(4):
                data[pl.ds(base + c * cap, 1), :] = picked[c][k : k + 1, :]
        return 0

    lax.fori_loop(0, scan_local, one_scan, 0)


def meet_all(n_grp, devices, me):
    barrier = pltpu.get_barrier_semaphore()

    def hello(k, _):
        peer = lax.rem(me + k, devices)
        pl.semaphore_signal(
            barrier, inc=1, device_id=(peer // n_grp, peer % n_grp), device_id_type=pl.DeviceIdType.MESH
        )
        return 0

    lax.fori_loop(1, devices, hello, 0)
    pl.semaphore_wait(barrier, devices - 1)


def remote(src, dst, send, recv, peer, n_grp):
    return pltpu.make_async_remote_copy(
        src_ref=src, dst_ref=dst, send_sem=send, recv_sem=recv,
        device_id=(peer // n_grp, peer % n_grp), device_id_type=pl.DeviceIdType.MESH,
    )


def exclusive(a, b, size):
    if size & (size - 1):
        return lax.rem(a + b, size)
    total = 0
    for bit in range(size.bit_length() - 1):
        total = total + ((((a >> bit) + (b >> bit)) & 1) << bit)
    return total


def split(values):
    high = values.astype(jnp.bfloat16)
    return high, (values - high.astype(jnp.float32)).astype(jnp.bfloat16)


def contract(a, b):
    return lax.dot_general(a, b, (((1,), (1,)), ((), ())), preferred_element_type=jnp.float32)


def row_sum(products):
    return jnp.sum(products, axis=0, keepdims=True)


def exchange_kernel(
    cap, n_grp, samples, count, data, meta, by_source, by_partner, shares,
    data_in, meta_in, codes, tiles, comps, turned, ids, result, packed,
    send_data, recv_data, send_meta, recv_meta, send_src, recv_src, send_part, recv_part,
    send_share, recv_share, own,
):
    scan_local, tiles_local = samples.shape[0], samples.shape[2]
    n_scan = send_src.shape[0]
    devices = n_scan * n_grp
    rows = cap * 4
    width = n_grp * cap
    per_block = LANES // width
    blocks = n_scan // per_block
    sources = per_block * n_grp
    packed_rows = packed.shape[1]
    scan_index, group_index = lax.axis_index("scan"), lax.axis_index("grp")
    me = scan_index * n_grp + group_index
    home, home_row = scan_index // per_block, lax.rem(scan_index, per_block)
    full_groups = min(LEAST_POINTS // (tiles_local * LANES), n_grp) if 3 * cap % 8 == 0 else 0
    short = rows - cap

    def send_one(src, dst_index, send_index, recv_index, peer, size):
        return remote(
            data.at[pl.ds(pl.multiple_of(src * rows, 8), size)],
            data_in.at[pl.ds(pl.multiple_of(dst_index * rows, 8), size)],
            send_data.at[send_index], recv_data.at[recv_index], peer, n_grp,
        )

    def send_code(src, dst_index, send_index, recv_index, peer):
        return remote(
            meta.at[src], meta_in.at[dst_index], send_meta.at[send_index], recv_meta.at[recv_index], peer, n_grp
        )

    def to_source(row, holder, index):
        peer = row * n_grp + home
        return remote(packed.at[row], by_source.at[holder], send_src.at[row], recv_src.at[index], peer, n_grp)

    def to_partner(block, at):
        peer = scan_index * n_grp + block
        return remote(result.at[block], by_partner.at[at], send_part.at[block], recv_part.at[at], peer, n_grp)

    def to_share(g, at):
        peer = scan_index * n_grp + g
        return remote(shares.at[group_index], shares.at[at], send_share.at[g], recv_share.at[at], peer, n_grp)

    meet_all(n_grp, devices, me)

    def start_meta(k, _):
        peer = lax.rem(me + k, devices)
        send_code(peer, me, peer, me, peer).start()
        return 0

    def wait_meta(k, _):
        peer = lax.rem(me + k, devices)
        copy = send_code(peer, peer, peer, peer, peer)
        copy.wait_send()
        copy.wait_recv()
        return 0

    def start_data(k, _):
        row = exclusive(scan_index, n_scan - 1 - k, n_scan)
        for g in range(n_grp):
            peer = row * n_grp + g

            @pl.when((peer != me) & (group_index < full_groups))
            def _():
                send_one(peer, me, peer, me, peer, short).start()

            @pl.when((peer != me) & (group_index >= full_groups))
            def _():
                send_one(peer, me, peer, me, peer, rows).start()

        return 0

    lax.fori_loop(1, devices, start_meta, 0)
    lax.fori_loop(0, n_scan, start_data, 0)
    own_data = pltpu.make_async_copy(
        data.at[pl.ds(pl.multiple_of(me * rows, 8), rows)], data_in.at[pl.ds(pl.multiple_of(me * rows, 8), rows)], own.at[0]
    )
    own_meta = pltpu.make_async_copy(meta.at[me], meta_in.at[me], own.at[1])
    own_data.start()
    own_meta.start()
    own_data.wait()
    own_meta.wait()

    def no_mask(row, _):
        for g in range(full_groups):
            first = pl.multiple_of((row * n_grp + g) * rows + short, 8)
            data_in[pl.ds(first, cap), :] = jnp.ones((cap, LANES), jnp.float32)
        return 0

    lax.fori_loop(0, n_scan, no_mask, 0)
    shares[...] = jnp.zeros_like(shares)
    result[...] = jnp.zeros_like(result)

    point = lax.broadcasted_iota(jnp.int32, (tiles_local, LANES), 0) * LANES
    point = point + lax.broadcasted_iota(jnp.int32, (tiles_local, LANES), 1)

    tile_rows = tiles.reshape(scan_local * tiles_local * 8, LANES)

    def fill(b, _):
        valid = point < count[b] - group_index * tiles_local * LANES
        for c in range(6):
            values = samples[b, c]
            if c >= 3:
                values = jnp.where(valid, values, 0.0)
            tile_rows[pl.ds(b * tiles_local * 8 + c, tiles_local, stride=8), :] = values
        return 0

    lax.fori_loop(0, scan_local, fill, 0)
    lax.fori_loop(1, devices, wait_meta, 0)
    to_scalar = pltpu.make_async_copy(meta_in, codes, own.at[2])
    to_scalar.start()

    slot_lane = lax.broadcasted_iota(jnp.int32, (sources, LANES), 1) // cap
    slot_row = lax.broadcasted_iota(jnp.int32, (sources, LANES), 0)

    def decode(m, _):
        arrived = meta_in[pl.ds(m * sources, sources), 0, :]
        kinds = []
        for kind in (0, 2):
            moved = pltpu.roll(arrived, LANES - kind * cap, 1) if kind else arrived
            moved = pltpu.roll(moved, 0, 1, stride=cap, stride_axis=0)
            kinds.append(row_sum(jnp.where(slot_lane == slot_row, moved, 0)))
        partner, source = kinds
        ids[m, 0:1, :] = source.astype(jnp.float32)
        ids[m, 1:2, :] = jnp.where(partner < 0, -1, scan_index * scan_local + partner).astype(jnp.float32)
        return 0

    lax.fori_loop(0, blocks, decode, 0)
    to_scalar.wait()

    def one_block(k, _):
        m = exclusive(home, blocks - 1 - k, blocks)

        def gather(i, _):
            for j in range(cap):
                slot = i * cap + j
                row = codes[m * sources + i, 0, cap + j]
                comps[pl.ds(pl.multiple_of(slot * 8, 8), 8), :] = tiles[row]
            return 0

        lax.fori_loop(0, sources, gather, 0)
        for c in range(6):
            turned[4 + c] = comps[pl.ds(c, LANES, stride=8), :].T

        def arrive(i, _):
            source = m * sources + i
            group = lax.rem(i, n_grp)

            @pl.when((source != me) & (group < full_groups))
            def _():
                send_one(source, source, source, source, source, short).wait_recv()

            @pl.when((source != me) & (group >= full_groups))
            def _():
                send_one(source, source, source, source, source, rows).wait_recv()

            return 0

        lax.fori_loop(0, sources, arrive, 0)
        for c in range(4):
            pieces = [
                data_in[pl.ds((m * sources + i) * rows + c * cap, cap), :] for i in range(sources)
            ]
            turned[c] = jnp.concatenate(pieces, axis=0).T

        def step(kk, sums):
            at = pl.ds(pl.multiple_of(kk * 8, 8), 8)
            px, py, pz, mask, qx, qy, qz, nx, ny, nz = [turned[c, at, :] for c in range(10)]
            residual = nx * (px - qx) + ny * (py - qy) + nz * (pz - qz)
            weight = mask / (1.0 + residual * residual)
            jac = [py * nz - pz * ny, pz * nx - px * nz, px * ny - py * nx, nx, ny, nz]
            scaled = [weight * x for x in jac]
            products = [scaled[a] * jac[b] for a, b in PAIRS] + [x * residual for x in scaled]
            return tuple(s + p for s, p in zip(sums, products))

        zero = jnp.zeros((8, LANES), jnp.float32)
        sums = lax.fori_loop(0, LANES // 8, step, (zero,) * (len(PAIRS) + 6))
        for q, total in enumerate(sums):
            result[m, q : q + 1, :] = row_sum(total)
        result[m, 27:29, :] = ids[m, 0:2, :]
        values = result[m]
        lane = lax.broadcasted_iota(jnp.int32, (packed_rows, LANES), 1) // width
        chunks = [values[g * packed_rows : (g + 1) * packed_rows, :] for g in range(per_block)]
        for p in range(per_block):
            total = chunks[p]
            for g in range(per_block):
                if g != p:
                    total = jnp.where(lane == g, pltpu.roll(chunks[g], (g - p) * width % LANES, 1), total)
            row = m * per_block + p
            packed[row] = total
            holder = group_index * per_block + home_row

            @pl.when(row * n_grp + home == me)
            def _():
                by_source[holder] = total

            @pl.when(row * n_grp + home != me)
            def _():
                to_source(row, holder, holder).start()

        @pl.when(m == group_index)
        def _():
            by_partner[group_index] = values

        @pl.when(m != group_index)
        def _():
            to_partner(m, group_index).start()

        return 0

    lax.fori_loop(0, blocks, one_block, 0)

    for holder in range(sources):
        group, other = holder // per_block, holder % per_block
        peer = (group_index * per_block + other) * n_grp + group

        @pl.when(peer != me)
        def _():
            to_source(0, holder, holder).wait_recv()

    for g in range(n_grp):

        @pl.when(g != group_index)
        def _():
            to_partner(0, g).wait_recv()

    span = lax.broadcasted_iota(jnp.int32, (2 * scan_local, LANES), 0)
    values, chosen = [], []
    for g in range(n_grp):
        parts = [by_source[g * per_block + p] for p in range(per_block)]
        block = jnp.concatenate(regroup(parts, width), axis=0)
        values.append(block)
        at = block[27:28, :].astype(jnp.int32) - scan_index * scan_local
        chosen.append(jnp.where(span == at, 1.0, 0.0))
    for g in range(n_grp):
        block = by_partner[g]
        values.append(block)
        at = block[28:29, :].astype(jnp.int32) - scan_index * scan_local
        chosen.append(jnp.where((at >= 0) & (span - scan_local == at), 1.0, 0.0))
    high, low = split(jnp.concatenate(values, axis=1))
    matrix = jnp.concatenate(chosen, axis=1).astype(jnp.bfloat16)
    shares[group_index, :, 0 : 2 * scan_local] = contract(high, matrix) + contract(low, matrix)
    for g in range(n_grp):

        @pl.when(g != group_index)
        def _():
            to_share(g, group_index).start()

    def finish(k, _):
        peer = lax.rem(me + k, devices)

        @pl.when(group_index < full_groups)
        def _():
            send_one(peer, peer, peer, peer, peer, short).wait_send()

        @pl.when(group_index >= full_groups)
        def _():
            send_one(peer, peer, peer, peer, peer, rows).wait_send()

        return 0

    lax.fori_loop(1, devices, finish, 0)

    def finish_source(row, _):
        @pl.when(row * n_grp + home != me)
        def _():
            to_source(row, 0, 0).wait_send()

        return 0

    lax.fori_loop(0, n_scan, finish_source, 0)
    for g in range(n_grp):

        @pl.when(g != group_index)
        def _():
            to_partner(g, 0).wait_send()
            copy = to_share(g, g)
            copy.wait_send()
            copy.wait_recv()


def regroup(parts, width):
    groups = len(parts)
    lane = lax.broadcasted_iota(jnp.int32, parts[0].shape, 1) // width
    out = []
    for b in range(groups):
        total = parts[b]
        for g in range(groups):
            if g != b:
                total = jnp.where(lane == g, pltpu.roll(parts[g], (g - b) * width % LANES, 1), total)
        out.append(total)
    return out


def assemble_kernel(n_grp, width, by_source, by_partner, shares, hessian, gradient, spare):
    rows, columns = hessian.shape[2], hessian.shape[3]
    grad_rows = gradient.shape[0]
    per_block = LANES // width
    scan_index, group_index = lax.axis_index("scan"), lax.axis_index("grp")
    home, home_row = scan_index // per_block, lax.rem(scan_index, per_block)
    first_row, first_column = scan_index * rows, group_index * columns
    count = len(PAIRS)

    share = shares[0]
    for g in range(1, n_grp):
        share = share + shares[g]
    other = pltpu.roll(share, LANES - rows, 1)
    spare[...] = (share - other).T
    gradient[...] = spare[pl.ds(group_index * grad_rows, grad_rows), 21:27]

    pieces = []
    for g in range(n_grp):
        parts = [by_source[g * per_block + p] for p in range(per_block)]
        block = jnp.concatenate(regroup(parts, width), axis=0)
        source, partner = block[27:28, :].astype(jnp.int32), block[28:29, :].astype(jnp.int32)
        pieces.append((block, source - first_row, partner - first_column))
    for g in range(n_grp):
        block = by_partner[g]
        source, partner = block[27:28, :].astype(jnp.int32), block[28:29, :].astype(jnp.int32)
        pieces.append((block, partner - first_row, source - first_column))
    lane = lax.broadcasted_iota(jnp.int32, (1, LANES), 1)
    diagonal = jnp.where((lane < rows) & (group_index == home), lane, -1)
    pieces.append((share + other, diagonal, jnp.where(diagonal < 0, -1, lane + home_row * rows)))

    left, right = [], []
    row = lax.broadcasted_iota(jnp.int32, (rows, LANES), 0)
    column = lax.broadcasted_iota(jnp.int32, (columns, LANES), 0)
    for index, (block, at, to) in enumerate(pieces):
        hit = row == at
        left.append(jnp.concatenate([jnp.where(hit, block[q : q + 1, :], 0.0) for q in range(count)], axis=0))
        right.append(jnp.where(column == to, 1.0 if index == 2 * n_grp else -1.0, 0.0))
    matrix = jnp.concatenate(right, axis=1).astype(jnp.bfloat16)
    high, low = split(jnp.concatenate(left, axis=1))
    total = contract(high, matrix) + contract(low, matrix)
    where = {pair: q for q, pair in enumerate(PAIRS)}
    for i in range(6):
        for j in range(6):
            q = where[min(i, j), max(i, j)]
            hessian[i, j] = total[q * rows : (q + 1) * rows, :]


def local(samples, point_count, corr_scan, corr_tile, corr_src):
    f32, i32 = jnp.float32, jnp.int32
    scan_local, tiles_local = samples.shape[0], samples.shape[1]
    request_count = scan_local * corr_scan.shape[1]
    n_scan, n_grp = lax.axis_size("scan"), lax.axis_size("grp")
    devices = n_scan * n_grp
    cap = 2 * request_count // devices
    width = n_grp * cap
    packed_rows = VALUES * width // LANES
    per_block = LANES // width
    blocks = n_scan // per_block
    columns = scan_local * n_scan // n_grp
    grad_rows = scan_local // n_grp
    assert blocks == n_grp and blocks * per_block == n_scan and 2 * scan_local <= LANES
    shape = jax.ShapeDtypeStruct
    dma = pltpu.SemaphoreType.DMA

    tiles = samples.transpose(0, 2, 1, 3)
    data, meta = pl.pallas_call(
        functools.partial(pack_kernel, cap, n_grp),
        out_shape=(shape((devices * cap * 4, LANES), f32), shape((devices, 1, LANES), i32)),
        in_specs=[VMEM, SMEM, SMEM, SMEM, VMEM],
        out_specs=(VMEM, SMEM),
        scratch_shapes=[pltpu.SMEM((devices,), i32)],
    )(tiles, point_count, corr_scan, corr_tile, corr_src)

    by_source, by_partner, shares = pl.pallas_call(
        functools.partial(exchange_kernel, cap, n_grp),
        out_shape=(
            shape((n_grp * per_block, packed_rows, LANES), f32),
            shape((n_grp, VALUES, LANES), f32),
            shape((n_grp, VALUES, LANES), f32),
        ),
        in_specs=[VMEM, SMEM, VMEM, VMEM],
        out_specs=(VMEM, VMEM, VMEM),
        scratch_shapes=[
            pltpu.VMEM(data.shape, f32),
            pltpu.VMEM(meta.shape, i32),
            pltpu.SMEM(meta.shape, i32),
            pltpu.VMEM((scan_local * tiles_local, 8, LANES), f32),
            pltpu.VMEM((LANES * 8, LANES), f32),
            pltpu.VMEM((10, LANES, LANES), f32),
            pltpu.VMEM((blocks, 8, LANES), f32),
            pltpu.VMEM((blocks, VALUES, LANES), f32),
            pltpu.VMEM((n_scan, packed_rows, LANES), f32),
        ]
        + [dma((devices,))] * 4
        + [dma((n_scan,)), dma((n_grp * per_block,))]
        + [dma((n_grp,))] * 4
        + [dma((3,))],
        compiler_params=pltpu.CompilerParams(collective_id=0, has_side_effects=True),
    )(tiles, point_count, data, meta)

    hessian, gradient = pl.pallas_call(
        functools.partial(assemble_kernel, n_grp, width),
        out_shape=(shape((6, 6, scan_local, columns), f32), shape((grad_rows, 6), f32)),
        in_specs=[VMEM, VMEM, VMEM],
        out_specs=(VMEM, VMEM),
        scratch_shapes=[pltpu.VMEM((LANES, VALUES), f32)],
    )(by_source, by_partner, shares)
    return hessian.transpose(2, 0, 1, 3), gradient


def solution(mesh):
    placed = (
        P("scan", "grp", None, None),
        P("scan"),
        P("scan", "grp"),
        P("scan", "grp"),
        P("scan", "grp", None),
    )
    return jax.shard_map(
        local,
        mesh=mesh,
        in_specs=placed,
        out_specs=(P("scan", None, None, "grp"), P(("scan", "grp"), None)),
        check_vma=False,
    )
```

time: 63.8 us -> 53.3 us (0.84)
  Pallas kernels: 63 us -> 52.5 us
    pallas_call x1, Pallas kernels: 7.69 us -> 2.29 us  [local(): pl.pallas_call(functools.partial(assemble_kernel, n_grp, width), out_shap...]
    pallas_call x1, Pallas kernels: 48.6 us -> 43.4 us  [local(): pl.pallas_call(functools.partial(exchange_kernel, cap, n_grp), out_shape=...]
where the time goes in v1:
time: 53.3 us; the launch traced here: 53.1 us
  Pallas kernels  52.5 us (98%)
  between operations  0.65 us (1%)
    pallas_call x1, Pallas kernels, local(): pl.pallas_call(functools.partial(exchange_kernel, cap, n_grp), out_shape=...  43.4 us
    pallas_call x1, Pallas kernels, local(): pl.pallas_call(functools.partial(pack_kernel, cap, n_grp), out_shape=(sha...  6.8 us
    pallas_call x1, Pallas kernels, local(): pl.pallas_call(functools.partial(assemble_kernel, n_grp, width), out_shap...  2.29 us

profile of v1, /device:TPU:0, one launch (start us, length us, event | category | flops | bytes accessed | tf_op | source)
XLA Modules:
  0.0 53.1 jit_solution(16153463375141489344)
XLA Ops:
  0.6 6.8 %shard_map.68 = (f32[2048,128]{1,0:T(8,128)}, s32[32,1,128]{2,1,0:T(1,128)}) custom-call(f32[16,6,16,128]{3,2,1,0:T(8,128)} %bitcast.2, s32[16]{0:T(128)} %count.3, s32[16,16]{1,0:T(8,128)} %corr_scan.1, s32[16,16]{1,0:T(8,128)} %corr_tile.1, s32[16,16,128]{2,1,0:T(8,128)} %corr_src.1), custom_call_target="tpu_custom_call" | custom-call | tf_op jit(solution)/shard_map/pallas_call | solution.py:478
  7.4 43.4 %shard_map.69 = (f32[8,16,128]{2,1,0:T(8,128)}, f32[4,32,128]{2,1,0:T(8,128)}, f32[4,32,128]{2,1,0:T(8,128)}) custom-call(f32[16,6,16,128]{3,2,1,0:T(8,128)} %bitcast.3, s32[16]{0:T(128)} %count.3, f32[2048,128]{1,0:T(8,128)} %get-tuple-element.9.data, s32[32,1,128]{2,1,0:T(1,128)} %get-tuple-element.10.meta), custom_call_target="tpu_custom_call" | custom-call | tf_op jit(solution)/shard_map/pallas_call | solution.py:486
  50.8 2.3 %shard_map.70 = (f32[6,6,16,32]{3,2,1,0:T(8,128)}, f32[4,6]{1,0:T(4,128)}) custom-call(f32[8,16,128]{2,1,0:T(8,128)} %get-tuple-element.11.by_source, f32[4,32,128]{2,1,0:T(8,128)} %get-tuple-element.12.by_partner, f32[4,32,128]{2,1,0:T(8,128)} %get-tuple-element.13.shares), custom_call_target="tpu_custom_call" | custom-call | tf_op jit(solution)/shard_map/pallas_call | solution.py:513

commit v2 on v1

--- a/solution.py
+++ b/solution.py
@@ -13,6 +13,7 @@
 PAIRS = [(i, j) for i in range(6) for j in range(i, 6)]
 VMEM = pl.BlockSpec(memory_space=pltpu.VMEM)
 SMEM = pl.BlockSpec(memory_space=pltpu.SMEM)
+ANY = pl.BlockSpec(memory_space=pl.ANY)
 
 
 def halves(value, size):
@@ -25,53 +26,76 @@
     return jnp.take_along_axis(table, index, axis=1, mode="promise_in_bounds")
 
 
-def pack_kernel(cap, n_grp, samples, count, corr_scan, corr_tile, corr_src, data, meta, used):
-    scan_local, tiles_local = samples.shape[0], samples.shape[2]
-    per_scan = corr_src.shape[1]
-    devices = meta.shape[0]
-    scan_index, group_index = lax.axis_index("scan"), lax.axis_index("grp")
-    first_point = group_index * tiles_local * LANES
-
-    def clear(d, _):
-        used[d] = 0
-        for j in range(cap):
-            meta[d, 0, j] = -1
-            meta[d, 0, cap + j] = 0
-            meta[d, 0, 2 * cap + j] = -1
-        data[pl.ds(pl.multiple_of(d * cap * 4, 8), cap * 4), :] = jnp.zeros((cap * 4, LANES), jnp.float32)
-        return 0
-
-    lax.fori_loop(0, devices, clear, 0)
-
-    def one_scan(s, _):
-        wanted = corr_src[s]
-        tile, lane = wanted >> 7, wanted & (LANES - 1)
-        picked = [jnp.zeros((per_scan, LANES), jnp.float32)] * 3
-        for t in range(tiles_local):
-            hit = tile == t
-            for c in range(3):
-                row = jnp.broadcast_to(samples[s, c, pl.ds(t, 1), :], (per_scan, LANES))
-                picked[c] = jnp.where(hit, lane_take(row, lane), picked[c])
-        mask = jnp.where(first_point + wanted < count[s], 1.0, 0.0).astype(jnp.float32)
-        picked.append(mask)
-        for k in range(per_scan):
-            b, t = corr_scan[s, k], corr_tile[s, k]
-            (b_dev, b_loc), (t_dev, t_loc) = halves(b, scan_local), halves(t, tiles_local)
-            d = b_dev * n_grp + t_dev
-            j = used[d]
-            used[d] = j + 1
-            meta[d, 0, j] = b_loc
-            meta[d, 0, cap + j] = b_loc * tiles_local + t_loc
-            meta[d, 0, 2 * cap + j] = scan_index * scan_local + s
-            base = d * cap * 4 + j
-            for c in range(4):
-                data[pl.ds(base + c * cap, 1), :] = picked[c][k : k + 1, :]
-        return 0
-
-    lax.fori_loop(0, scan_local, one_scan, 0)
-
-
-def meet_all(n_grp, devices, me):
+def route_kernel(cap, n_grp, scan_local, tiles_local, corr_scan, corr_tile, slots, meta, wide):
+    per_scan = corr_scan.shape[1]
+    scan_index = lax.axis_index("scan")
+    requests = scan_local * per_scan
+    chunks, together = requests // LANES, LANES // per_scan
+    f32 = jnp.float32
+
+    def flat(ref):
+        wide[...] = jnp.zeros_like(wide)
+        wide[:, 0:per_scan] = ref[...]
+        out = []
+        for h in range(chunks):
+            moved = pltpu.roll(wide[h * together : (h + 1) * together, :], 0, 1, stride=per_scan, stride_axis=0)
+            out.append(row_sum(moved))
+        return out
+
+    def column(row):
+        return jnp.broadcast_to(row, (LANES, LANES)).T
+
+    scans, tiles = flat(corr_scan), flat(corr_tile)
+    sublane = lax.broadcasted_iota(jnp.int32, (LANES, LANES), 0)
+    lane = lax.broadcasted_iota(jnp.int32, (LANES, LANES), 1)
+    targets, locals_, flats = [], [], []
+    for b, t in zip(scans, tiles):
+        (b_dev, b_loc), (t_dev, t_loc) = halves(b, scan_local), halves(t, tiles_local)
+        targets.append((b_dev * n_grp + t_dev).astype(f32))
+        locals_.append(b_loc.astype(f32))
+        flats.append((b_loc * tiles_local + t_loc).astype(f32))
+    target_columns = [column(x) for x in targets]
+    places = []
+    for h in range(chunks):
+        rank = jnp.zeros((1, LANES), f32)
+        for e in range(h + 1):
+            same = target_columns[e] == targets[h]
+            if e == h:
+                same = same & (sublane < lane)
+            rank = rank + row_sum(jnp.where(same, 1.0, 0.0))
+        places.append(column(targets[h] * cap + rank))
+    blank = jnp.zeros((4, LANES), f32)
+    one = jnp.ones((1, LANES), f32)
+    index = lax.broadcasted_iota(jnp.int32, (1, LANES), 1).astype(f32)
+    left = jnp.concatenate(
+        [
+            jnp.concatenate([one, index + h * LANES, locals_[h], flats[h], blank], axis=0) for h in range(chunks)
+        ],
+        axis=1,
+    ).astype(jnp.bfloat16)
+    served = LANES // cap
+    for a in range(slots.shape[0]):
+        hits = [jnp.where(places[h] == (lane + a * LANES).astype(f32), 1.0, 0.0) for h in range(chunks)]
+        table = lax.dot_general(
+            left, jnp.concatenate(hits, axis=0).astype(jnp.bfloat16), (((1,), (0,)), ((), ())),
+            preferred_element_type=f32,
+        ).astype(jnp.int32)
+        used, request = table[0:1, :] > 0, table[1:2, :]
+        slots[a : a + 1, :] = request
+        source = scan_index * scan_local + halves(request, per_scan)[0]
+        kinds = [jnp.where(used, table[2:3, :], -1), table[3:4, :], jnp.where(used, source, -1)]
+        total = jnp.zeros((served, LANES), jnp.int32)
+        part = lax.broadcasted_iota(jnp.int32, (served, LANES), 1) // cap
+        for kind, row in enumerate(kinds):
+            moved = pltpu.roll(jnp.broadcast_to(row, (served, LANES)), cap, 1, stride=cap, stride_axis=0)
+            if kind:
+                moved = pltpu.roll(moved, kind * cap, 1)
+            total = jnp.where(part == kind, moved, total)
+        for i in range(served):
+            meta[a * served + i] = total[served - 1 - i : served - i, :]
+
+
+def greet_all(n_grp, devices, me):
     barrier = pltpu.get_barrier_semaphore()
 
     def hello(k, _):
@@ -82,7 +106,10 @@
         return 0
 
     lax.fori_loop(1, devices, hello, 0)
-    pl.semaphore_wait(barrier, devices - 1)
+
+
+def await_all(devices):
+    pl.semaphore_wait(pltpu.get_barrier_semaphore(), devices - 1)
 
 
 def remote(src, dst, send, recv, peer, n_grp):
@@ -115,12 +142,13 @@
 
 
 def exchange_kernel(
-    cap, n_grp, samples, count, data, meta, by_source, by_partner, shares,
-    data_in, meta_in, codes, tiles, comps, turned, ids, result, packed,
+    cap, n_grp, samples_hbm, count_hbm, wanted_hbm, slots_hbm, meta, by_source, by_partner, shares,
+    samples, count, wanted, slots, picks, data, data_in, meta_in, codes, tiles, comps, turned, ids, result, packed,
     send_data, recv_data, send_meta, recv_meta, send_src, recv_src, send_part, recv_part,
     send_share, recv_share, own,
 ):
     scan_local, tiles_local = samples.shape[0], samples.shape[2]
+    per_scan = wanted.shape[1]
     n_scan = send_src.shape[0]
     devices = n_scan * n_grp
     rows = cap * 4
@@ -159,7 +187,45 @@
         peer = scan_index * n_grp + g
         return remote(shares.at[group_index], shares.at[at], send_share.at[g], recv_share.at[at], peer, n_grp)
 
-    meet_all(n_grp, devices, me)
+    greet_all(n_grp, devices, me)
+    fetch = pltpu.make_async_copy(samples_hbm, samples, own.at[3])
+    fetch_count = pltpu.make_async_copy(count_hbm, count, own.at[4])
+    fetch_wanted = pltpu.make_async_copy(wanted_hbm, wanted, own.at[0])
+    fetch_slots = pltpu.make_async_copy(slots_hbm, slots, own.at[2])
+    fetch_count.start()
+    fetch_slots.start()
+    fetch_wanted.start()
+    fetch.start()
+    fetch_count.wait()
+    fetch_wanted.wait()
+    fetch.wait()
+    pick_rows = picks.reshape(scan_local * per_scan * 8, LANES)
+    first_point = group_index * tiles_local * LANES
+
+    def pick(s, _):
+        point = wanted[s]
+        tile, place = point >> 7, point & (LANES - 1)
+        picked = [jnp.zeros((per_scan, LANES), jnp.float32)] * 3
+        for t in range(tiles_local):
+            hit = tile == t
+            for c in range(3):
+                row = jnp.broadcast_to(samples[s, c, pl.ds(t, 1), :], (per_scan, LANES))
+                picked[c] = jnp.where(hit, lane_take(row, place), picked[c])
+        picked.append(jnp.where(first_point + point < count[s], 1.0, 0.0).astype(jnp.float32))
+        for c in range(4):
+            pick_rows[pl.ds(s * per_scan * 8 + c, per_scan, stride=8), :] = picked[c]
+        return 0
+
+    lax.fori_loop(0, scan_local, pick, 0)
+    fetch_slots.wait()
+
+    def collect(peer, into):
+        first = lax.rem(peer, LANES // cap) * cap
+        for j in range(cap):
+            request = slots[peer // (LANES // cap), first + j]
+            into[pl.ds(peer * rows + j, 4, stride=cap), :] = picks[request, 0:4, :]
+
+    await_all(devices)
 
     def start_meta(k, _):
         peer = lax.rem(me + k, devices)
@@ -176,7 +242,9 @@
     def start_data(k, _):
         row = exclusive(scan_index, n_scan - 1 - k, n_scan)
         for g in range(n_grp):
-            peer = row * n_grp + g
+            collect(row * n_grp + exclusive(group_index, g, n_grp), data)
+        for g in range(n_grp):
+            peer = row * n_grp + exclusive(group_index, g, n_grp)
 
             @pl.when((peer != me) & (group_index < full_groups))
             def _():
@@ -190,13 +258,9 @@
 
     lax.fori_loop(1, devices, start_meta, 0)
     lax.fori_loop(0, n_scan, start_data, 0)
-    own_data = pltpu.make_async_copy(
-        data.at[pl.ds(pl.multiple_of(me * rows, 8), rows)], data_in.at[pl.ds(pl.multiple_of(me * rows, 8), rows)], own.at[0]
-    )
     own_meta = pltpu.make_async_copy(meta.at[me], meta_in.at[me], own.at[1])
-    own_data.start()
     own_meta.start()
-    own_data.wait()
+    collect(me, data_in)
     own_meta.wait()
 
     def no_mask(row, _):
@@ -475,13 +539,15 @@
     dma = pltpu.SemaphoreType.DMA
 
     tiles = samples.transpose(0, 2, 1, 3)
-    data, meta = pl.pallas_call(
-        functools.partial(pack_kernel, cap, n_grp),
-        out_shape=(shape((devices * cap * 4, LANES), f32), shape((devices, 1, LANES), i32)),
-        in_specs=[VMEM, SMEM, SMEM, SMEM, VMEM],
-        out_specs=(VMEM, SMEM),
-        scratch_shapes=[pltpu.SMEM((devices,), i32)],
-    )(tiles, point_count, corr_scan, corr_tile, corr_src)
+    per_scan = corr_scan.shape[1]
+    assert request_count <= 256 and scan_local * tiles_local <= 256
+    slots, meta = pl.pallas_call(
+        functools.partial(route_kernel, cap, n_grp, scan_local, tiles_local),
+        out_shape=(shape((devices * cap // LANES, LANES), i32), shape((devices, 1, LANES), i32)),
+        in_specs=[VMEM, VMEM],
+        out_specs=(VMEM, VMEM),
+        scratch_shapes=[pltpu.VMEM((scan_local, LANES), i32)],
+    )(corr_scan, corr_tile)
 
     by_source, by_partner, shares = pl.pallas_call(
         functools.partial(exchange_kernel, cap, n_grp),
@@ -490,10 +556,16 @@
             shape((n_grp, VALUES, LANES), f32),
             shape((n_grp, VALUES, LANES), f32),
         ),
-        in_specs=[VMEM, SMEM, VMEM, VMEM],
+        in_specs=[ANY] * 5,
         out_specs=(VMEM, VMEM, VMEM),
         scratch_shapes=[
-            pltpu.VMEM(data.shape, f32),
+            pltpu.VMEM(tiles.shape, f32),
+            pltpu.SMEM(point_count.shape, i32),
+            pltpu.VMEM(corr_src.shape, i32),
+            pltpu.SMEM(slots.shape, i32),
+            pltpu.VMEM((request_count, 8, LANES), f32),
+            pltpu.VMEM((devices * cap * 4, LANES), f32),
+            pltpu.VMEM((devices * cap * 4, LANES), f32),
             pltpu.VMEM(meta.shape, i32),
             pltpu.SMEM(meta.shape, i32),
             pltpu.VMEM((scan_local * tiles_local, 8, LANES), f32),
@@ -506,9 +578,9 @@
         + [dma((devices,))] * 4
         + [dma((n_scan,)), dma((n_grp * per_block,))]
         + [dma((n_grp,))] * 4
-        + [dma((3,))],
+        + [dma((5,))],
         compiler_params=pltpu.CompilerParams(collective_id=0, has_side_effects=True),
-    )(tiles, point_count, data, meta)
+    )(tiles, point_count, corr_src, slots, meta)
 
     hessian, gradient = pl.pallas_call(
         functools.partial(assemble_kernel, n_grp, width),

time: 53.3 us -> 49.6 us (0.931)
  Pallas kernels: 52.5 us -> 48.6 us
    pallas_call x1, Pallas kernels: 6.8 us -> 1.9 us  [local(): pl.pallas_call(functools.partial(route_kernel, cap, n_grp, scan_local, ti...]
    pallas_call x1, Pallas kernels: 43.4 us -> 44.4 us  [local(): pl.pallas_call(functools.partial(exchange_kernel, cap, n_grp), out_shape=...]
where the time goes in v2:
time: 49.6 us; the launch traced here: 49.3 us
  Pallas kernels  48.6 us (98%)
  between operations  0.64 us (1%)
    pallas_call x1, Pallas kernels, local(): pl.pallas_call(functools.partial(exchange_kernel, cap, n_grp), out_shape=...  44.4 us
    pallas_call x1, Pallas kernels, local(): pl.pallas_call(functools.partial(assemble_kernel, n_grp, width), out_shap...  2.29 us
    pallas_call x1, Pallas kernels, local(): pl.pallas_call(functools.partial(route_kernel, cap, n_grp, scan_local, ti...  1.9 us

profile of v2, /device:TPU:0, one launch (start us, length us, event | category | flops | bytes accessed | tf_op | source)
XLA Modules:
  0.0 49.3 jit_solution(2668996584523916282)
XLA Ops:
  0.6 1.9 %shard_map.68 = (s32[4,128]{1,0:T(4,128)}, s32[32,1,128]{2,1,0:T(1,128)}) custom-call(s32[16,16]{1,0:T(8,128)} %corr_scan.1, s32[16,16]{1,0:T(8,128)} %corr_tile.1), custom_call_target="tpu_custom_call" | custom-call | tf_op jit(solution)/shard_map/pallas_call | solution.py:544
  2.5 44.4 %shard_map.69 = (f32[8,16,128]{2,1,0:T(8,128)}, f32[4,32,128]{2,1,0:T(8,128)}, f32[4,32,128]{2,1,0:T(8,128)}) custom-call(f32[16,6,16,128]{3,2,1,0:T(8,128)} %bitcast.2, s32[16]{0:T(128)} %count_hbm.1, s32[16,16,128]{2,1,0:T(8,128)} %wanted_hbm.1, s32[4,128]{1,0:T(4,128)} %get-tuple-element.9.slots_hbm, s32[32,1,128]{2,1,0:T(1,128)} %get-tuple-element.10.meta), custom_call_target="tpu_custom_call" | custom-call | tf_op jit(solution)/shard_map/pallas_call | solution.py:552
  47.0 2.3 %shard_map.70 = (f32[6,6,16,32]{3,2,1,0:T(8,128)}, f32[4,6]{1,0:T(4,128)}) custom-call(f32[8,16,128]{2,1,0:T(8,128)} %get-tuple-element.11.by_source, f32[4,32,128]{2,1,0:T(8,128)} %get-tuple-element.12.by_partner, f32[4,32,128]{2,1,0:T(8,128)} %get-tuple-element.13.shares), custom_call_target="tpu_custom_call" | custom-call | tf_op jit(solution)/shard_map/pallas_call | solution.py:585

commit v3 on v2

--- a/solution.py
+++ b/solution.py
@@ -240,10 +240,10 @@
         return 0
 
     def start_data(k, _):
-        row = exclusive(scan_index, n_scan - 1 - k, n_scan)
-        for g in range(n_grp):
+        row = exclusive(scan_index, k + 1 - 2 * (k & 1), n_scan)
+        for g in reversed(range(n_grp)):
             collect(row * n_grp + exclusive(group_index, g, n_grp), data)
-        for g in range(n_grp):
+        for g in reversed(range(n_grp)):
             peer = row * n_grp + exclusive(group_index, g, n_grp)
 
             @pl.when((peer != me) & (group_index < full_groups))
@@ -311,7 +311,7 @@
     to_scalar.wait()
 
     def one_block(k, _):
-        m = exclusive(home, blocks - 1 - k, blocks)
+        m = exclusive(home, k, blocks)
 
         def gather(i, _):
             for j in range(cap):

time: 49.6 us -> 46.7 us (0.942)
  the two profiles are of different devices: /device:TPU:0 before, /device:TPU:9 now
where the time goes in v3:
time: 46.7 us; the launch traced here: 46.4 us
  Pallas kernels  45.8 us (98%)
  between operations  0.64 us (1%)
    pallas_call x1, Pallas kernels, local(): pl.pallas_call(functools.partial(exchange_kernel, cap, n_grp), out_shape=...  41.6 us
    pallas_call x1, Pallas kernels, local(): pl.pallas_call(functools.partial(assemble_kernel, n_grp, width), out_shap...  2.3 us
    pallas_call x1, Pallas kernels, local(): pl.pallas_call(functools.partial(route_kernel, cap, n_grp, scan_local, ti...  1.9 us

profile of v3, /device:TPU:9, one launch (start us, length us, event | category | flops | bytes accessed | tf_op | source)
XLA Modules:
  0.0 46.4 jit_solution(9819802607661426669)
XLA Ops:
  0.6 1.9 %shard_map.68 = (s32[4,128]{1,0:T(4,128)}, s32[32,1,128]{2,1,0:T(1,128)}) custom-call(s32[16,16]{1,0:T(8,128)} %corr_scan.1, s32[16,16]{1,0:T(8,128)} %corr_tile.1), custom_call_target="tpu_custom_call" | custom-call | tf_op jit(solution)/shard_map/pallas_call | solution.py:544
  2.5 41.6 %shard_map.69 = (f32[8,16,128]{2,1,0:T(8,128)}, f32[4,32,128]{2,1,0:T(8,128)}, f32[4,32,128]{2,1,0:T(8,128)}) custom-call(f32[16,6,16,128]{3,2,1,0:T(8,128)} %bitcast.2, s32[16]{0:T(128)} %count_hbm.1, s32[16,16,128]{2,1,0:T(8,128)} %wanted_hbm.1, s32[4,128]{1,0:T(4,128)} %get-tuple-element.9.slots_hbm, s32[32,1,128]{2,1,0:T(1,128)} %get-tuple-element.10.meta), custom_call_target="tpu_custom_call" | custom-call | tf_op jit(solution)/shard_map/pallas_call | solution.py:552
  44.1 2.3 %shard_map.70 = (f32[6,6,16,32]{3,2,1,0:T(8,128)}, f32[4,6]{1,0:T(4,128)}) custom-call(f32[8,16,128]{2,1,0:T(8,128)} %get-tuple-element.11.by_source, f32[4,32,128]{2,1,0:T(8,128)} %get-tuple-element.12.by_partner, f32[4,32,128]{2,1,0:T(8,128)} %get-tuple-element.13.shares), custom_call_target="tpu_custom_call" | custom-call | tf_op jit(solution)/shard_map/pallas_call | solution.py:585

commit v4 on v3

--- a/solution.py
+++ b/solution.py
@@ -10,6 +10,8 @@
 LANES = 128
 VALUES = 32
 LEAST_POINTS = 4096
+SUMS = VALUES // 8
+IDS, VECTOR = 21, 24
 PAIRS = [(i, j) for i in range(6) for j in range(i, 6)]
 VMEM = pl.BlockSpec(memory_space=pltpu.VMEM)
 SMEM = pl.BlockSpec(memory_space=pltpu.SMEM)
@@ -141,15 +143,32 @@
     return jnp.sum(products, axis=0, keepdims=True)
 
 
+def wait_for(ref, count, semaphore):
+    part = ref.at[pl.ds(0, count)]
+    pltpu.make_async_copy(part, part, semaphore).wait()
+
+
+def compact(sums, place, rows):
+    lane = lax.broadcasted_iota(jnp.int32, (8, LANES), 1)
+    out = []
+    for a in range(SUMS):
+        part = sums[a * 8 : (a + 1) * 8, :]
+        if place:
+            part = pltpu.roll(part, LANES - place * rows, 1)
+        part = jnp.where(lane < rows, part, 0.0)
+        out.append(row_sum(pltpu.roll(part, 0, 1, stride=rows, stride_axis=0)))
+    return out
+
+
 def exchange_kernel(
-    cap, n_grp, samples_hbm, count_hbm, wanted_hbm, slots_hbm, meta, by_source, by_partner, shares,
+    cap, n_grp, samples_hbm, count_hbm, wanted_hbm, slots_hbm, meta, by_source, by_partner, shares, parts,
     samples, count, wanted, slots, picks, data, data_in, meta_in, codes, tiles, comps, turned, ids, result, packed,
-    send_data, recv_data, send_meta, recv_meta, send_src, recv_src, send_part, recv_part,
-    send_share, recv_share, own,
+    tally, share_out, part_out,
+    sent, received, recv_data, own,
 ):
     scan_local, tiles_local = samples.shape[0], samples.shape[2]
     per_scan = wanted.shape[1]
-    n_scan = send_src.shape[0]
+    n_scan = packed.shape[0]
     devices = n_scan * n_grp
     rows = cap * 4
     width = n_grp * cap
@@ -163,31 +182,38 @@
     full_groups = min(LEAST_POINTS // (tiles_local * LANES), n_grp) if 3 * cap % 8 == 0 else 0
     short = rows - cap
 
-    def send_one(src, dst_index, send_index, recv_index, peer, size):
+    def send_one(peer, size):
         return remote(
-            data.at[pl.ds(pl.multiple_of(src * rows, 8), size)],
-            data_in.at[pl.ds(pl.multiple_of(dst_index * rows, 8), size)],
-            send_data.at[send_index], recv_data.at[recv_index], peer, n_grp,
+            data.at[pl.ds(pl.multiple_of(peer * rows, 8), size)],
+            data_in.at[pl.ds(pl.multiple_of(me * rows, 8), size)],
+            sent.at[0], recv_data.at[home], peer, n_grp,
         )
 
-    def send_code(src, dst_index, send_index, recv_index, peer):
+    def send_code(peer):
+        return remote(meta.at[peer], meta_in.at[me], sent.at[1], received.at[1], peer, n_grp)
+
+    def to_source(row, holder):
+        peer = row * n_grp + home
+        return remote(packed.at[row], by_source.at[holder], sent.at[2], received.at[2], peer, n_grp)
+
+    def to_partner(block):
+        peer = scan_index * n_grp + block
+        return remote(result.at[block], by_partner.at[group_index], sent.at[3], received.at[3], peer, n_grp)
+
+    def to_share(peer, row, first):
+        size = SUMS - first
         return remote(
-            meta.at[src], meta_in.at[dst_index], send_meta.at[send_index], recv_meta.at[recv_index], peer, n_grp
+            share_out.at[pl.ds(row * SUMS + first, size)], shares.at[pl.ds(me * SUMS + first, size)],
+            sent.at[4], received.at[4], peer, n_grp,
         )
 
-    def to_source(row, holder, index):
-        peer = row * n_grp + home
-        return remote(packed.at[row], by_source.at[holder], send_src.at[row], recv_src.at[index], peer, n_grp)
-
-    def to_partner(block, at):
-        peer = scan_index * n_grp + block
-        return remote(result.at[block], by_partner.at[at], send_part.at[block], recv_part.at[at], peer, n_grp)
-
-    def to_share(g, at):
-        peer = scan_index * n_grp + g
-        return remote(shares.at[group_index], shares.at[at], send_share.at[g], recv_share.at[at], peer, n_grp)
-
-    greet_all(n_grp, devices, me)
+    def to_part(g, first):
+        size = SUMS - first
+        return remote(
+            part_out.at[pl.ds(first, size)], parts.at[pl.ds(group_index * SUMS + first, size)],
+            sent.at[5], received.at[5], scan_index * n_grp + g, n_grp,
+        )
+
     fetch = pltpu.make_async_copy(samples_hbm, samples, own.at[3])
     fetch_count = pltpu.make_async_copy(count_hbm, count, own.at[4])
     fetch_wanted = pltpu.make_async_copy(wanted_hbm, wanted, own.at[0])
@@ -196,6 +222,7 @@
     fetch_slots.start()
     fetch_wanted.start()
     fetch.start()
+    greet_all(n_grp, devices, me)
     fetch_count.wait()
     fetch_wanted.wait()
     fetch.wait()
@@ -216,7 +243,7 @@
             pick_rows[pl.ds(s * per_scan * 8 + c, per_scan, stride=8), :] = picked[c]
         return 0
 
-    lax.fori_loop(0, scan_local, pick, 0)
+    lax.fori_loop(0, scan_local, pick, 0, unroll=2)
     fetch_slots.wait()
 
     def collect(peer, into):
@@ -229,14 +256,7 @@
 
     def start_meta(k, _):
         peer = lax.rem(me + k, devices)
-        send_code(peer, me, peer, me, peer).start()
-        return 0
-
-    def wait_meta(k, _):
-        peer = lax.rem(me + k, devices)
-        copy = send_code(peer, peer, peer, peer, peer)
-        copy.wait_send()
-        copy.wait_recv()
+        send_code(peer).start()
         return 0
 
     def start_data(k, _):
@@ -248,11 +268,11 @@
 
             @pl.when((peer != me) & (group_index < full_groups))
             def _():
-                send_one(peer, me, peer, me, peer, short).start()
+                send_one(peer, short).start()
 
             @pl.when((peer != me) & (group_index >= full_groups))
             def _():
-                send_one(peer, me, peer, me, peer, rows).start()
+                send_one(peer, rows).start()
 
         return 0
 
@@ -270,7 +290,7 @@
         return 0
 
     lax.fori_loop(0, n_scan, no_mask, 0)
-    shares[...] = jnp.zeros_like(shares)
+    tally[...] = jnp.zeros_like(tally)
     result[...] = jnp.zeros_like(result)
 
     point = lax.broadcasted_iota(jnp.int32, (tiles_local, LANES), 0) * LANES
@@ -288,7 +308,7 @@
         return 0
 
     lax.fori_loop(0, scan_local, fill, 0)
-    lax.fori_loop(1, devices, wait_meta, 0)
+    wait_for(meta_in, devices - 1, received.at[1])
     to_scalar = pltpu.make_async_copy(meta_in, codes, own.at[2])
     to_scalar.start()
 
@@ -324,21 +344,20 @@
         for c in range(6):
             turned[4 + c] = comps[pl.ds(c, LANES, stride=8), :].T
 
-        def arrive(i, _):
-            source = m * sources + i
-            group = lax.rem(i, n_grp)
-
-            @pl.when((source != me) & (group < full_groups))
-            def _():
-                send_one(source, source, source, source, source, short).wait_recv()
-
-            @pl.when((source != me) & (group >= full_groups))
-            def _():
-                send_one(source, source, source, source, source, rows).wait_recv()
-
-            return 0
-
-        lax.fori_loop(0, sources, arrive, 0)
+        whole = per_block * (n_grp * rows - full_groups * cap)
+
+        @pl.when(m != home)
+        def _():
+            wait_for(data_in, whole, recv_data.at[m])
+
+        @pl.when((m == home) & (group_index < full_groups))
+        def _():
+            wait_for(data_in, whole - short, recv_data.at[m])
+
+        @pl.when((m == home) & (group_index >= full_groups))
+        def _():
+            wait_for(data_in, whole - rows, recv_data.at[m])
+
         for c in range(4):
             pieces = [
                 data_in[pl.ds((m * sources + i) * rows + c * cap, cap), :] for i in range(sources)
@@ -358,8 +377,9 @@
         zero = jnp.zeros((8, LANES), jnp.float32)
         sums = lax.fori_loop(0, LANES // 8, step, (zero,) * (len(PAIRS) + 6))
         for q, total in enumerate(sums):
+            q = q if q < len(PAIRS) else q - len(PAIRS) + VECTOR
             result[m, q : q + 1, :] = row_sum(total)
-        result[m, 27:29, :] = ids[m, 0:2, :]
+        result[m, IDS : IDS + 2, :] = ids[m, 0:2, :]
         values = result[m]
         lane = lax.broadcasted_iota(jnp.int32, (packed_rows, LANES), 1) // width
         chunks = [values[g * packed_rows : (g + 1) * packed_rows, :] for g in range(per_block)]
@@ -374,91 +394,99 @@
 
             @pl.when(row * n_grp + home == me)
             def _():
-                by_source[holder] = total
+                pltpu.make_async_copy(packed.at[row], by_source.at[holder], own.at[3]).start()
 
             @pl.when(row * n_grp + home != me)
             def _():
-                to_source(row, holder, holder).start()
+                to_source(row, holder).start()
 
         @pl.when(m == group_index)
         def _():
-            by_partner[group_index] = values
+            pltpu.make_async_copy(result.at[group_index], by_partner.at[group_index], own.at[4]).start()
 
         @pl.when(m != group_index)
         def _():
-            to_partner(m, group_index).start()
+            to_partner(m).start()
+
+        high, low = split(values)
+        source = ids[m, 0:1, :].astype(jnp.int32) - m * per_block * scan_local
+        partner = ids[m, 1:2, :].astype(jnp.int32) - scan_index * scan_local
+        span = lax.broadcasted_iota(jnp.int32, (LANES, LANES), 0)
+        chosen = jnp.where(span == source, 1.0, 0.0).astype(jnp.bfloat16)
+        sums = contract(high, chosen) + contract(low, chosen)
+        chosen = jnp.where(span == partner, 1.0, 0.0).astype(jnp.bfloat16)
+        tally[...] += contract(high, chosen) + contract(low, chosen)
+        for p in range(per_block):
+            row = m * per_block + p
+            for a, line in enumerate(compact(sums, p, scan_local)):
+                share_out[row * SUMS + a] = line
+            for g in range(n_grp):
+                peer = row * n_grp + g
+
+                @pl.when((peer != me) & (m == g))
+                def _():
+                    to_share(peer, row, 0).start()
+
+                @pl.when((peer != me) & (m != g))
+                def _():
+                    to_share(peer, row, SUMS - 1).start()
 
         return 0
 
     lax.fori_loop(0, blocks, one_block, 0)
-
-    for holder in range(sources):
-        group, other = holder // per_block, holder % per_block
-        peer = (group_index * per_block + other) * n_grp + group
-
-        @pl.when(peer != me)
+    for a, line in enumerate(compact(tally[...], 0, scan_local)):
+        part_out[a] = line
+    own_share = pltpu.make_async_copy(
+        share_out.at[pl.ds(scan_index * SUMS, SUMS)], shares.at[pl.ds(me * SUMS, SUMS)], own.at[0]
+    )
+    own_part = pltpu.make_async_copy(part_out, parts.at[pl.ds(group_index * SUMS, SUMS)], own.at[1])
+    own_share.start()
+    own_part.start()
+    for g in range(n_grp):
+
+        @pl.when((g != group_index) & (home == g))
         def _():
-            to_source(0, holder, holder).wait_recv()
-
-    for g in range(n_grp):
-
-        @pl.when(g != group_index)
+            to_part(g, 0).start()
+
+        @pl.when((g != group_index) & (home != g))
         def _():
-            to_partner(0, g).wait_recv()
-
-    span = lax.broadcasted_iota(jnp.int32, (2 * scan_local, LANES), 0)
-    values, chosen = [], []
-    for g in range(n_grp):
-        parts = [by_source[g * per_block + p] for p in range(per_block)]
-        block = jnp.concatenate(regroup(parts, width), axis=0)
-        values.append(block)
-        at = block[27:28, :].astype(jnp.int32) - scan_index * scan_local
-        chosen.append(jnp.where(span == at, 1.0, 0.0))
-    for g in range(n_grp):
-        block = by_partner[g]
-        values.append(block)
-        at = block[28:29, :].astype(jnp.int32) - scan_index * scan_local
-        chosen.append(jnp.where((at >= 0) & (span - scan_local == at), 1.0, 0.0))
-    high, low = split(jnp.concatenate(values, axis=1))
-    matrix = jnp.concatenate(chosen, axis=1).astype(jnp.bfloat16)
-    shares[group_index, :, 0 : 2 * scan_local] = contract(high, matrix) + contract(low, matrix)
-    for g in range(n_grp):
-
-        @pl.when(g != group_index)
-        def _():
-            to_share(g, group_index).start()
-
-    def finish(k, _):
-        peer = lax.rem(me + k, devices)
-
-        @pl.when(group_index < full_groups)
-        def _():
-            send_one(peer, peer, peer, peer, peer, short).wait_send()
-
-        @pl.when(group_index >= full_groups)
-        def _():
-            send_one(peer, peer, peer, peer, peer, rows).wait_send()
-
-        return 0
-
-    lax.fori_loop(1, devices, finish, 0)
-
-    def finish_source(row, _):
-        @pl.when(row * n_grp + home != me)
-        def _():
-            to_source(row, 0, 0).wait_send()
-
-        return 0
-
-    lax.fori_loop(0, n_scan, finish_source, 0)
-    for g in range(n_grp):
-
-        @pl.when(g != group_index)
-        def _():
-            to_partner(g, 0).wait_send()
-            copy = to_share(g, g)
-            copy.wait_send()
-            copy.wait_recv()
+            to_part(g, SUMS - 1).start()
+
+    others = n_grp - 1
+    wait_for(by_partner, others, received.at[3])
+    wait_for(result, others, sent.at[3])
+    wait_for(meta_in, devices - 1, sent.at[1])
+
+    @pl.when(home == group_index)
+    def _():
+        pltpu.make_async_copy(packed.at[0], by_source.at[0], own.at[3]).wait()
+        wait_for(by_source, sources - 1, received.at[2])
+        wait_for(packed, n_scan - 1, sent.at[2])
+        wait_for(shares, (devices - 1) * SUMS, received.at[4])
+        wait_for(shares, n_scan * (SUMS + others) - SUMS, sent.at[4])
+        wait_for(parts, others * SUMS, received.at[5])
+        wait_for(parts, others, sent.at[5])
+
+    @pl.when(home != group_index)
+    def _():
+        wait_for(by_source, sources, received.at[2])
+        wait_for(packed, n_scan, sent.at[2])
+        wait_for(shares, devices - 1, received.at[4])
+        wait_for(shares, n_scan * (SUMS + others) - 1, sent.at[4])
+        wait_for(parts, others, received.at[5])
+        wait_for(parts, others - 1 + SUMS, sent.at[5])
+
+    pltpu.make_async_copy(result.at[0], by_partner.at[group_index], own.at[4]).wait()
+    own_share.wait()
+    own_part.wait()
+
+    @pl.when(group_index < full_groups)
+    def _():
+        wait_for(data, (devices - 1) * short, sent.at[0])
+
+    @pl.when(group_index >= full_groups)
+    def _():
+        wait_for(data, (devices - 1) * rows, sent.at[0])
 
 
 def regroup(parts, width):
@@ -474,7 +502,7 @@
     return out
 
 
-def assemble_kernel(n_grp, width, by_source, by_partner, shares, hessian, gradient, spare):
+def assemble_kernel(n_grp, width, by_source, by_partner, shares, parts, hessian, gradient, spare):
     rows, columns = hessian.shape[2], hessian.shape[3]
     grad_rows = gradient.shape[0]
     per_block = LANES // width
@@ -483,33 +511,43 @@
     first_row, first_column = scan_index * rows, group_index * columns
     count = len(PAIRS)
 
-    share = shares[0]
-    for g in range(1, n_grp):
-        share = share + shares[g]
-    other = pltpu.roll(share, LANES - rows, 1)
-    spare[...] = (share - other).T
-    gradient[...] = spare[pl.ds(group_index * grad_rows, grad_rows), 21:27]
+    def total_of(ref):
+        total = ref[0:SUMS, 0, :]
+        for d in range(1, ref.shape[0] // SUMS):
+            total = total + ref[d * SUMS : (d + 1) * SUMS, 0, :]
+        return total
+
+    def spread(line):
+        return pltpu.roll(jnp.broadcast_to(line, (8, LANES)), rows, 1, stride=rows, stride_axis=0)
+
+    outgoing, incoming = total_of(shares), total_of(parts)
+    vector = spread(outgoing[SUMS - 1 :, :] - incoming[SUMS - 1 :, :])
+    spare[...] = jnp.concatenate([vector[7 - i : 8 - i, :] for i in range(8)], axis=0).T
+    gradient[...] = spare[pl.ds(group_index * grad_rows, grad_rows), 0:6]
+    both = [spread(outgoing[a : a + 1, :] + incoming[a : a + 1, :]) for a in range(SUMS - 1)]
+    lines = [both[q // 8][7 - q % 8 : 8 - q % 8, :] for q in range(count)]
 
     pieces = []
     for g in range(n_grp):
-        parts = [by_source[g * per_block + p] for p in range(per_block)]
-        block = jnp.concatenate(regroup(parts, width), axis=0)
-        source, partner = block[27:28, :].astype(jnp.int32), block[28:29, :].astype(jnp.int32)
+        halves_ = [by_source[g * per_block + p] for p in range(per_block)]
+        block = jnp.concatenate(regroup(halves_, width), axis=0)
+        source, partner = [block[r : r + 1, :].astype(jnp.int32) for r in (IDS, IDS + 1)]
         pieces.append((block, source - first_row, partner - first_column))
     for g in range(n_grp):
         block = by_partner[g]
-        source, partner = block[27:28, :].astype(jnp.int32), block[28:29, :].astype(jnp.int32)
+        source, partner = [block[r : r + 1, :].astype(jnp.int32) for r in (IDS, IDS + 1)]
         pieces.append((block, partner - first_row, source - first_column))
+    pieces = [([block[q : q + 1, :] for q in range(count)], at, to) for block, at, to in pieces]
     lane = lax.broadcasted_iota(jnp.int32, (1, LANES), 1)
     diagonal = jnp.where((lane < rows) & (group_index == home), lane, -1)
-    pieces.append((share + other, diagonal, jnp.where(diagonal < 0, -1, lane + home_row * rows)))
+    pieces.append((lines, diagonal, jnp.where(diagonal < 0, -1, lane + home_row * rows)))
 
     left, right = [], []
     row = lax.broadcasted_iota(jnp.int32, (rows, LANES), 0)
     column = lax.broadcasted_iota(jnp.int32, (columns, LANES), 0)
     for index, (block, at, to) in enumerate(pieces):
         hit = row == at
-        left.append(jnp.concatenate([jnp.where(hit, block[q : q + 1, :], 0.0) for q in range(count)], axis=0))
+        left.append(jnp.concatenate([jnp.where(hit, block[q], 0.0) for q in range(count)], axis=0))
         right.append(jnp.where(column == to, 1.0 if index == 2 * n_grp else -1.0, 0.0))
     matrix = jnp.concatenate(right, axis=1).astype(jnp.bfloat16)
     high, low = split(jnp.concatenate(left, axis=1))
@@ -534,7 +572,7 @@
     blocks = n_scan // per_block
     columns = scan_local * n_scan // n_grp
     grad_rows = scan_local // n_grp
-    assert blocks == n_grp and blocks * per_block == n_scan and 2 * scan_local <= LANES
+    assert blocks == n_grp and blocks * per_block == n_scan and 8 * scan_local == LANES
     shape = jax.ShapeDtypeStruct
     dma = pltpu.SemaphoreType.DMA
 
@@ -549,15 +587,16 @@
         scratch_shapes=[pltpu.VMEM((scan_local, LANES), i32)],
     )(corr_scan, corr_tile)
 
-    by_source, by_partner, shares = pl.pallas_call(
+    by_source, by_partner, shares, parts = pl.pallas_call(
         functools.partial(exchange_kernel, cap, n_grp),
         out_shape=(
             shape((n_grp * per_block, packed_rows, LANES), f32),
             shape((n_grp, VALUES, LANES), f32),
-            shape((n_grp, VALUES, LANES), f32),
+            shape((devices * SUMS, 1, LANES), f32),
+            shape((n_grp * SUMS, 1, LANES), f32),
         ),
         in_specs=[ANY] * 5,
-        out_specs=(VMEM, VMEM, VMEM),
+        out_specs=(ANY,) * 4,
         scratch_shapes=[
             pltpu.VMEM(tiles.shape, f32),
             pltpu.SMEM(point_count.shape, i32),
@@ -574,21 +613,21 @@
             pltpu.VMEM((blocks, 8, LANES), f32),
             pltpu.VMEM((blocks, VALUES, LANES), f32),
             pltpu.VMEM((n_scan, packed_rows, LANES), f32),
+            pltpu.VMEM((VALUES, LANES), f32),
+            pltpu.VMEM((n_scan * SUMS, 1, LANES), f32),
+            pltpu.VMEM((SUMS, 1, LANES), f32),
         ]
-        + [dma((devices,))] * 4
-        + [dma((n_scan,)), dma((n_grp * per_block,))]
-        + [dma((n_grp,))] * 4
-        + [dma((5,))],
+        + [dma((6,)), dma((6,)), dma((blocks,)), dma((5,))],
         compiler_params=pltpu.CompilerParams(collective_id=0, has_side_effects=True),
     )(tiles, point_count, corr_src, slots, meta)
 
     hessian, gradient = pl.pallas_call(
         functools.partial(assemble_kernel, n_grp, width),
         out_shape=(shape((6, 6, scan_local, columns), f32), shape((grad_rows, 6), f32)),
-        in_specs=[VMEM, VMEM, VMEM],
+        in_specs=[VMEM] * 4,
         out_specs=(VMEM, VMEM),
-        scratch_shapes=[pltpu.VMEM((LANES, VALUES), f32)],
-    )(by_source, by_partner, shares)
+        scratch_shapes=[pltpu.VMEM((LANES, 8), f32)],
+    )(by_source, by_partner, shares, parts)
     return hessian.transpose(2, 0, 1, 3), gradient
 
 

time: 46.7 us -> 42.5 us (0.910)
  Pallas kernels: 45.8 us -> 41.6 us
    pallas_call x1, Pallas kernels: 41.6 us -> 37.4 us  [local(): pl.pallas_call(functools.partial(exchange_kernel, cap, n_grp), out_shape=...]
where the time goes in v4:
time: 42.5 us; the launch traced here: 42.2 us
  Pallas kernels  41.6 us (98%)
  between operations  0.64 us (2%)
    pallas_call x1, Pallas kernels, local(): pl.pallas_call(functools.partial(exchange_kernel, cap, n_grp), out_shape=...  37.4 us
    pallas_call x1, Pallas kernels, local(): pl.pallas_call(functools.partial(assemble_kernel, n_grp, width), out_shap...  2.29 us
    pallas_call x1, Pallas kernels, local(): pl.pallas_call(functools.partial(route_kernel, cap, n_grp, scan_local, ti...  1.9 us

profile of v4, /device:TPU:9, one launch (start us, length us, event | category | flops | bytes accessed | tf_op | source)
XLA Modules:
  0.0 42.2 jit_solution(3550082677172125836)
XLA Ops:
  0.6 1.9 %shard_map.68 = (s32[4,128]{1,0:T(4,128)}, s32[32,1,128]{2,1,0:T(1,128)}) custom-call(s32[16,16]{1,0:T(8,128)} %corr_scan.1, s32[16,16]{1,0:T(8,128)} %corr_tile.1), custom_call_target="tpu_custom_call" | custom-call | tf_op jit(solution)/shard_map/pallas_call | solution.py:582
  2.5 37.4 %shard_map.69 = (f32[8,16,128]{2,1,0:T(8,128)}, f32[4,32,128]{2,1,0:T(8,128)}, f32[128,1,128]{2,1,0:T(1,128)}, f32[16,1,128]{2,1,0:T(1,128)}) custom-call(f32[16,6,16,128]{3,2,1,0:T(8,128)} %bitcast.2, s32[16]{0:T(128)} %count_hbm.1, s32[16,16,128]{2,1,0:T(8,128)} %wanted_hbm.1, s32[4,128]{1,0:T(4,128)} %get-tuple-element.10.slots_hbm, ...), custom_call_target="tpu_custom_call" | custom-call | tf_op jit(solution)/shard_map/pallas_call | solution.py:590
  39.9 2.3 %shard_map.70 = (f32[6,6,16,32]{3,2,1,0:T(8,128)}, f32[4,6]{1,0:T(4,128)}) custom-call(f32[8,16,128]{2,1,0:T(8,128)} %get-tuple-element.12.by_source, f32[4,32,128]{2,1,0:T(8,128)} %get-tuple-element.13.by_partner, f32[128,1,128]{2,1,0:T(1,128)} %get-tuple-element.14.shares, f32[16,1,128]{2,1,0:T(1,128)} %get-tuple-element.15.parts), custom_call_target="tpu_custom_call" | custom-call | tf_op jit(solution)/shard_map/pallas_call | solution.py:624

commit v5 on v4

--- a/solution.py
+++ b/solution.py
@@ -162,7 +162,7 @@
 
 def exchange_kernel(
     cap, n_grp, samples_hbm, count_hbm, wanted_hbm, slots_hbm, meta, by_source, by_partner, shares, parts,
-    samples, count, wanted, slots, picks, data, data_in, meta_in, codes, tiles, comps, turned, ids, result, packed,
+    samples, count, wanted, slots, data, data_in, meta_in, codes, tiles, comps, turned, ids, result, packed,
     tally, share_out, part_out,
     sent, received, recv_data, own,
 ):
@@ -226,31 +226,24 @@
     fetch_count.wait()
     fetch_wanted.wait()
     fetch.wait()
-    pick_rows = picks.reshape(scan_local * per_scan * 8, LANES)
+    fetch_slots.wait()
     first_point = group_index * tiles_local * LANES
-
-    def pick(s, _):
-        point = wanted[s]
-        tile, place = point >> 7, point & (LANES - 1)
-        picked = [jnp.zeros((per_scan, LANES), jnp.float32)] * 3
-        for t in range(tiles_local):
-            hit = tile == t
-            for c in range(3):
-                row = jnp.broadcast_to(samples[s, c, pl.ds(t, 1), :], (per_scan, LANES))
-                picked[c] = jnp.where(hit, lane_take(row, place), picked[c])
-        picked.append(jnp.where(first_point + point < count[s], 1.0, 0.0).astype(jnp.float32))
-        for c in range(4):
-            pick_rows[pl.ds(s * per_scan * 8 + c, per_scan, stride=8), :] = picked[c]
-        return 0
-
-    lax.fori_loop(0, scan_local, pick, 0, unroll=2)
-    fetch_slots.wait()
+    wanted_rows = wanted.reshape(scan_local * per_scan, LANES)
+    tile_row = lax.broadcasted_iota(jnp.int32, (tiles_local, LANES), 0)
 
     def collect(peer, into):
         first = lax.rem(peer, LANES // cap) * cap
         for j in range(cap):
             request = slots[peer // (LANES // cap), first + j]
-            into[pl.ds(peer * rows + j, 4, stride=cap), :] = picks[request, 0:4, :]
+            s = halves(request, per_scan)[0]
+            point = wanted_rows[pl.ds(request, 1), :]
+            spread = jnp.broadcast_to(point, (tiles_local, LANES))
+            hit, place = spread >> 7 == tile_row, spread & (LANES - 1)
+            for c in range(3):
+                found = jnp.where(hit, lane_take(samples[s, c], place), 0.0)
+                into[pl.ds(peer * rows + c * cap + j, 1), :] = row_sum(found)
+            mask = jnp.where(first_point + point < count[s], 1.0, 0.0).astype(jnp.float32)
+            into[pl.ds(peer * rows + 3 * cap + j, 1), :] = mask
 
     await_all(devices)
 
@@ -260,24 +253,23 @@
         return 0
 
     def start_data(k, _):
-        row = exclusive(scan_index, k + 1 - 2 * (k & 1), n_scan)
-        for g in reversed(range(n_grp)):
-            collect(row * n_grp + exclusive(group_index, g, n_grp), data)
-        for g in reversed(range(n_grp)):
-            peer = row * n_grp + exclusive(group_index, g, n_grp)
-
-            @pl.when((peer != me) & (group_index < full_groups))
-            def _():
-                send_one(peer, short).start()
-
-            @pl.when((peer != me) & (group_index >= full_groups))
-            def _():
-                send_one(peer, rows).start()
+        peer = exclusive(me, k, devices)
+        collect(peer, data)
+
+        @pl.when((peer != me) & (group_index < full_groups))
+        def _():
+            send_one(peer, short).start()
+
+        @pl.when((peer != me) & (group_index >= full_groups))
+        def _():
+            send_one(peer, rows).start()
 
         return 0
 
     lax.fori_loop(1, devices, start_meta, 0)
-    lax.fori_loop(0, n_scan, start_data, 0)
+    share = devices // 4
+    for quarter in (2, 1, 3, 0):
+        lax.fori_loop(quarter * share, (quarter + 1) * share, start_data, 0)
     own_meta = pltpu.make_async_copy(meta.at[me], meta_in.at[me], own.at[1])
     own_meta.start()
     collect(me, data_in)
@@ -375,7 +367,7 @@
             return tuple(s + p for s, p in zip(sums, products))
 
         zero = jnp.zeros((8, LANES), jnp.float32)
-        sums = lax.fori_loop(0, LANES // 8, step, (zero,) * (len(PAIRS) + 6))
+        sums = lax.fori_loop(0, LANES // 8, step, (zero,) * (len(PAIRS) + 6), unroll=True)
         for q, total in enumerate(sums):
             q = q if q < len(PAIRS) else q - len(PAIRS) + VECTOR
             result[m, q : q + 1, :] = row_sum(total)
@@ -602,7 +594,6 @@
             pltpu.SMEM(point_count.shape, i32),
             pltpu.VMEM(corr_src.shape, i32),
             pltpu.SMEM(slots.shape, i32),
-            pltpu.VMEM((request_count, 8, LANES), f32),
             pltpu.VMEM((devices * cap * 4, LANES), f32),
             pltpu.VMEM((devices * cap * 4, LANES), f32),
             pltpu.VMEM(meta.shape, i32),

time: 42.5 us -> 40.3 us (0.948)
  Pallas kernels: 41.6 us -> 39.4 us
    pallas_call x1, Pallas kernels: 37.4 us -> 35.2 us  [local(): pl.pallas_call(functools.partial(exchange_kernel, cap, n_grp), out_shape=...]
where the time goes in v5:
time: 40.3 us; the launch traced here: 40 us
  Pallas kernels  39.4 us (98%)
  between operations  0.64 us (2%)
    pallas_call x1, Pallas kernels, local(): pl.pallas_call(functools.partial(exchange_kernel, cap, n_grp), out_shape=...  35.2 us
    pallas_call x1, Pallas kernels, local(): pl.pallas_call(functools.partial(assemble_kernel, n_grp, width), out_shap...  2.3 us
    pallas_call x1, Pallas kernels, local(): pl.pallas_call(functools.partial(route_kernel, cap, n_grp, scan_local, ti...  1.9 us

profile of v5, /device:TPU:9, one launch (start us, length us, event | category | flops | bytes accessed | tf_op | source)
XLA Modules:
  0.0 40.0 jit_solution(12120071610431221891)
XLA Ops:
  0.6 1.9 %shard_map.68 = (s32[4,128]{1,0:T(4,128)}, s32[32,1,128]{2,1,0:T(1,128)}) custom-call(s32[16,16]{1,0:T(8,128)} %corr_scan.1, s32[16,16]{1,0:T(8,128)} %corr_tile.1), custom_call_target="tpu_custom_call" | custom-call | tf_op jit(solution)/shard_map/pallas_call | solution.py:574
  2.5 35.2 %shard_map.69 = (f32[8,16,128]{2,1,0:T(8,128)}, f32[4,32,128]{2,1,0:T(8,128)}, f32[128,1,128]{2,1,0:T(1,128)}, f32[16,1,128]{2,1,0:T(1,128)}) custom-call(f32[16,6,16,128]{3,2,1,0:T(8,128)} %bitcast.2, s32[16]{0:T(128)} %count_hbm.1, s32[16,16,128]{2,1,0:T(8,128)} %wanted_hbm.1, s32[4,128]{1,0:T(4,128)} %get-tuple-element.10.slots_hbm, ...), custom_call_target="tpu_custom_call" | custom-call | tf_op jit(solution)/shard_map/pallas_call | solution.py:582
  37.7 2.3 %shard_map.70 = (f32[6,6,16,32]{3,2,1,0:T(8,128)}, f32[4,6]{1,0:T(4,128)}) custom-call(f32[8,16,128]{2,1,0:T(8,128)} %get-tuple-element.12.by_source, f32[4,32,128]{2,1,0:T(8,128)} %get-tuple-element.13.by_partner, f32[128,1,128]{2,1,0:T(1,128)} %get-tuple-element.14.shares, f32[16,1,128]{2,1,0:T(1,128)} %get-tuple-element.15.parts), custom_call_target="tpu_custom_call" | custom-call | tf_op jit(solution)/shard_map/pallas_call | solution.py:615

commit v6 on v5

--- a/solution.py
+++ b/solution.py
@@ -12,6 +12,7 @@
 LEAST_POINTS = 4096
 SUMS = VALUES // 8
 IDS, VECTOR = 21, 24
+FLAT, USED = 512, 1 << 20
 PAIRS = [(i, j) for i in range(6) for j in range(i, 6)]
 VMEM = pl.BlockSpec(memory_space=pltpu.VMEM)
 SMEM = pl.BlockSpec(memory_space=pltpu.SMEM)
@@ -28,12 +29,9 @@
     return jnp.take_along_axis(table, index, axis=1, mode="promise_in_bounds")
 
 
-def route_kernel(cap, n_grp, scan_local, tiles_local, corr_scan, corr_tile, slots, meta, wide):
-    per_scan = corr_scan.shape[1]
-    scan_index = lax.axis_index("scan")
-    requests = scan_local * per_scan
-    chunks, together = requests // LANES, LANES // per_scan
-    f32 = jnp.float32
+def route(cap, n_grp, tiles_local, first_scan, scans, tiles, wide, slots, meta):
+    scan_local, per_scan = scans.shape
+    chunks, together = scan_local * per_scan // LANES, LANES // per_scan
 
     def flat(ref):
         wide[...] = jnp.zeros_like(wide)
@@ -47,47 +45,35 @@
     def column(row):
         return jnp.broadcast_to(row, (LANES, LANES)).T
 
-    scans, tiles = flat(corr_scan), flat(corr_tile)
     sublane = lax.broadcasted_iota(jnp.int32, (LANES, LANES), 0)
     lane = lax.broadcasted_iota(jnp.int32, (LANES, LANES), 1)
-    targets, locals_, flats = [], [], []
-    for b, t in zip(scans, tiles):
+    index = lax.broadcasted_iota(jnp.int32, (1, LANES), 1)
+    targets, codes = [], []
+    for h, (b, t) in enumerate(zip(flat(scans), flat(tiles))):
         (b_dev, b_loc), (t_dev, t_loc) = halves(b, scan_local), halves(t, tiles_local)
-        targets.append((b_dev * n_grp + t_dev).astype(f32))
-        locals_.append(b_loc.astype(f32))
-        flats.append((b_loc * tiles_local + t_loc).astype(f32))
+        targets.append(b_dev * n_grp + t_dev)
+        codes.append(column(USED + (b_loc * tiles_local + t_loc) * FLAT + index + h * LANES))
     target_columns = [column(x) for x in targets]
     places = []
     for h in range(chunks):
-        rank = jnp.zeros((1, LANES), f32)
+        rank = jnp.zeros((1, LANES), jnp.int32)
         for e in range(h + 1):
             same = target_columns[e] == targets[h]
             if e == h:
                 same = same & (sublane < lane)
-            rank = rank + row_sum(jnp.where(same, 1.0, 0.0))
+            rank = rank + row_sum(jnp.where(same, 1, 0))
         places.append(column(targets[h] * cap + rank))
-    blank = jnp.zeros((4, LANES), f32)
-    one = jnp.ones((1, LANES), f32)
-    index = lax.broadcasted_iota(jnp.int32, (1, LANES), 1).astype(f32)
-    left = jnp.concatenate(
-        [
-            jnp.concatenate([one, index + h * LANES, locals_[h], flats[h], blank], axis=0) for h in range(chunks)
-        ],
-        axis=1,
-    ).astype(jnp.bfloat16)
     served = LANES // cap
+    part = lax.broadcasted_iota(jnp.int32, (served, LANES), 1) // cap
     for a in range(slots.shape[0]):
-        hits = [jnp.where(places[h] == (lane + a * LANES).astype(f32), 1.0, 0.0) for h in range(chunks)]
-        table = lax.dot_general(
-            left, jnp.concatenate(hits, axis=0).astype(jnp.bfloat16), (((1,), (0,)), ((), ())),
-            preferred_element_type=f32,
-        ).astype(jnp.int32)
-        used, request = table[0:1, :] > 0, table[1:2, :]
+        table = jnp.zeros((1, LANES), jnp.int32)
+        for h in range(chunks):
+            table = table + row_sum(jnp.where(places[h] == lane + a * LANES, codes[h], 0))
+        used, request, tile = table >= USED, table & (FLAT - 1), (table & (USED - 1)) >> (FLAT.bit_length() - 1)
         slots[a : a + 1, :] = request
-        source = scan_index * scan_local + halves(request, per_scan)[0]
-        kinds = [jnp.where(used, table[2:3, :], -1), table[3:4, :], jnp.where(used, source, -1)]
+        source = first_scan + halves(request, per_scan)[0]
+        kinds = [jnp.where(used, halves(tile, tiles_local)[0], -1), tile, jnp.where(used, source, -1)]
         total = jnp.zeros((served, LANES), jnp.int32)
-        part = lax.broadcasted_iota(jnp.int32, (served, LANES), 1) // cap
         for kind, row in enumerate(kinds):
             moved = pltpu.roll(jnp.broadcast_to(row, (served, LANES)), cap, 1, stride=cap, stride_axis=0)
             if kind:
@@ -141,6 +127,10 @@
 
 def row_sum(products):
     return jnp.sum(products, axis=0, keepdims=True)
+
+
+def within(index, size):
+    return jnp.maximum(jnp.minimum(index, size - 1), 0)
 
 
 def wait_for(ref, count, semaphore):
@@ -161,8 +151,8 @@
 
 
 def exchange_kernel(
-    cap, n_grp, samples_hbm, count_hbm, wanted_hbm, slots_hbm, meta, by_source, by_partner, shares, parts,
-    samples, count, wanted, slots, data, data_in, meta_in, codes, tiles, comps, turned, ids, result, packed,
+    cap, n_grp, samples_hbm, count_hbm, wanted_hbm, scans_hbm, tiles_hbm, by_source, by_partner, shares, parts,
+    samples, count, wanted, scans, partner_tiles, wide, routed, slots, meta, data, data_in, meta_in, codes, tiles, comps, turned, ids, result, packed,
     tally, share_out, part_out,
     sent, received, recv_data, own,
 ):
@@ -217,12 +207,19 @@
     fetch = pltpu.make_async_copy(samples_hbm, samples, own.at[3])
     fetch_count = pltpu.make_async_copy(count_hbm, count, own.at[4])
     fetch_wanted = pltpu.make_async_copy(wanted_hbm, wanted, own.at[0])
-    fetch_slots = pltpu.make_async_copy(slots_hbm, slots, own.at[2])
+    fetch_scans = pltpu.make_async_copy(scans_hbm, scans, own.at[1])
+    fetch_tiles = pltpu.make_async_copy(tiles_hbm, partner_tiles, own.at[2])
+    fetch_scans.start()
+    fetch_tiles.start()
     fetch_count.start()
-    fetch_slots.start()
     fetch_wanted.start()
     fetch.start()
     greet_all(n_grp, devices, me)
+    fetch_scans.wait()
+    fetch_tiles.wait()
+    route(cap, n_grp, tiles_local, scan_index * scan_local, scans, partner_tiles, wide, routed, meta)
+    fetch_slots = pltpu.make_async_copy(routed, slots, own.at[1])
+    fetch_slots.start()
     fetch_count.wait()
     fetch_wanted.wait()
     fetch.wait()
@@ -234,7 +231,7 @@
     def collect(peer, into):
         first = lax.rem(peer, LANES // cap) * cap
         for j in range(cap):
-            request = slots[peer // (LANES // cap), first + j]
+            request = within(slots[peer // (LANES // cap), first + j], scan_local * per_scan)
             s = halves(request, per_scan)[0]
             point = wanted_rows[pl.ds(request, 1), :]
             spread = jnp.broadcast_to(point, (tiles_local, LANES))
@@ -328,7 +325,7 @@
         def gather(i, _):
             for j in range(cap):
                 slot = i * cap + j
-                row = codes[m * sources + i, 0, cap + j]
+                row = within(codes[m * sources + i, 0, cap + j], scan_local * tiles_local)
                 comps[pl.ds(pl.multiple_of(slot * 8, 8), 8), :] = tiles[row]
             return 0
 
@@ -570,14 +567,8 @@
 
     tiles = samples.transpose(0, 2, 1, 3)
     per_scan = corr_scan.shape[1]
-    assert request_count <= 256 and scan_local * tiles_local <= 256
-    slots, meta = pl.pallas_call(
-        functools.partial(route_kernel, cap, n_grp, scan_local, tiles_local),
-        out_shape=(shape((devices * cap // LANES, LANES), i32), shape((devices, 1, LANES), i32)),
-        in_specs=[VMEM, VMEM],
-        out_specs=(VMEM, VMEM),
-        scratch_shapes=[pltpu.VMEM((scan_local, LANES), i32)],
-    )(corr_scan, corr_tile)
+    assert request_count <= FLAT and scan_local * tiles_local * FLAT <= USED
+    table = (devices * cap // LANES, LANES)
 
     by_source, by_partner, shares, parts = pl.pallas_call(
         functools.partial(exchange_kernel, cap, n_grp),
@@ -593,11 +584,16 @@
             pltpu.VMEM(tiles.shape, f32),
             pltpu.SMEM(point_count.shape, i32),
             pltpu.VMEM(corr_src.shape, i32),
-            pltpu.SMEM(slots.shape, i32),
+            pltpu.VMEM(corr_scan.shape, i32),
+            pltpu.VMEM(corr_tile.shape, i32),
+            pltpu.VMEM((scan_local, LANES), i32),
+            pltpu.VMEM(table, i32),
+            pltpu.SMEM(table, i32),
+            pltpu.VMEM((devices, 1, LANES), i32),
             pltpu.VMEM((devices * cap * 4, LANES), f32),
             pltpu.VMEM((devices * cap * 4, LANES), f32),
-            pltpu.VMEM(meta.shape, i32),
-            pltpu.SMEM(meta.shape, i32),
+            pltpu.VMEM((devices, 1, LANES), i32),
+            pltpu.SMEM((devices, 1, LANES), i32),
             pltpu.VMEM((scan_local * tiles_local, 8, LANES), f32),
             pltpu.VMEM((LANES * 8, LANES), f32),
             pltpu.VMEM((10, LANES, LANES), f32),
@@ -610,7 +606,7 @@
         ]
         + [dma((6,)), dma((6,)), dma((blocks,)), dma((5,))],
         compiler_params=pltpu.CompilerParams(collective_id=0, has_side_effects=True),
-    )(tiles, point_count, corr_src, slots, meta)
+    )(tiles, point_count, corr_src, corr_scan, corr_tile)
 
     hessian, gradient = pl.pallas_call(
         functools.partial(assemble_kernel, n_grp, width),

time: 40.3 us -> 38.5 us (0.955)
  Pallas kernels: 39.4 us -> 37.6 us
    pallas_call x1 -> x0, Pallas kernels: 1.9 us -> none  [local(): pl.pallas_call(functools.partial(route_kernel, cap, n_grp, scan_local, ti...]
where the time goes in v6:
time: 38.5 us; the launch traced here: 38.2 us
  Pallas kernels  37.6 us (98%)
  between operations  0.64 us (2%)
    pallas_call x1, Pallas kernels, local(): pl.pallas_call(functools.partial(exchange_kernel, cap, n_grp), out_shape=...  35.3 us
    pallas_call x1, Pallas kernels, local(): pl.pallas_call(functools.partial(assemble_kernel, n_grp, width), out_shap...  2.29 us

profile of v6, /device:TPU:9, one launch (start us, length us, event | category | flops | bytes accessed | tf_op | source)
XLA Modules:
  0.0 38.2 jit_solution(10033529321531856183)
XLA Ops:
  0.6 35.3 %shard_map.68 = (f32[8,16,128]{2,1,0:T(8,128)}, f32[4,32,128]{2,1,0:T(8,128)}, f32[128,1,128]{2,1,0:T(1,128)}, f32[16,1,128]{2,1,0:T(1,128)}) custom-call(f32[16,6,16,128]{3,2,1,0:T(8,128)} %bitcast.2, s32[16]{0:T(128)} %count_hbm.1, s32[16,16,128]{2,1,0:T(8,128)} %wanted_hbm.1, s32[16,16]{1,0:T(8,128)} %scans_hbm.1, s32[16,16]{1,0:T(8,128)} %tiles_hbm.1), custom_call_target="tpu_custom_call" | custom-call | tf_op jit(solution)/shard_map/pallas_call | solution.py:573
  36.0 2.3 %shard_map.69 = (f32[6,6,16,32]{3,2,1,0:T(8,128)}, f32[4,6]{1,0:T(4,128)}) custom-call(f32[8,16,128]{2,1,0:T(8,128)} %get-tuple-element.8.by_source, f32[4,32,128]{2,1,0:T(8,128)} %get-tuple-element.9.by_partner, f32[128,1,128]{2,1,0:T(1,128)} %get-tuple-element.10.shares, f32[16,1,128]{2,1,0:T(1,128)} %get-tuple-element.11.parts), custom_call_target="tpu_custom_call" | custom-call | tf_op jit(solution)/shard_map/pallas_call | solution.py:611

commit v7 on v6

--- a/solution.py
+++ b/solution.py
@@ -11,7 +11,7 @@
 VALUES = 32
 LEAST_POINTS = 4096
 SUMS = VALUES // 8
-IDS, VECTOR = 21, 24
+IDS, VECTOR, REPLY = 21, 24, 24
 FLAT, USED = 512, 1 << 20
 PAIRS = [(i, j) for i in range(6) for j in range(i, 6)]
 VMEM = pl.BlockSpec(memory_space=pltpu.VMEM)
@@ -556,7 +556,7 @@
     devices = n_scan * n_grp
     cap = 2 * request_count // devices
     width = n_grp * cap
-    packed_rows = VALUES * width // LANES
+    packed_rows = REPLY * width // LANES
     per_block = LANES // width
     blocks = n_scan // per_block
     columns = scan_local * n_scan // n_grp

time: 38.5 us -> 38.3 us (level)
  no operation moved by 1% of the time
where the time goes in v7:
time: 38.3 us; the launch traced here: 38.1 us
  Pallas kernels  37.5 us (98%)
  between operations  0.64 us (2%)
    pallas_call x1, Pallas kernels, local(): pl.pallas_call(functools.partial(exchange_kernel, cap, n_grp), out_shape=...  35.2 us
    pallas_call x1, Pallas kernels, local(): pl.pallas_call(functools.partial(assemble_kernel, n_grp, width), out_shap...  2.29 us

profile of v7, /device:TPU:9, one launch (start us, length us, event | category | flops | bytes accessed | tf_op | source)
XLA Modules:
  0.0 38.1 jit_solution(6135673055763899520)
XLA Ops:
  0.6 35.2 %shard_map.68 = (f32[8,12,128]{2,1,0:T(8,128)}, f32[4,32,128]{2,1,0:T(8,128)}, f32[128,1,128]{2,1,0:T(1,128)}, f32[16,1,128]{2,1,0:T(1,128)}) custom-call(f32[16,6,16,128]{3,2,1,0:T(8,128)} %bitcast.2, s32[16]{0:T(128)} %count_hbm.1, s32[16,16,128]{2,1,0:T(8,128)} %wanted_hbm.1, s32[16,16]{1,0:T(8,128)} %scans_hbm.1, s32[16,16]{1,0:T(8,128)} %tiles_hbm.1), custom_call_target="tpu_custom_call" | custom-call | tf_op jit(solution)/shard_map/pallas_call | solution.py:573
  35.8 2.3 %shard_map.69 = (f32[6,6,16,32]{3,2,1,0:T(8,128)}, f32[4,6]{1,0:T(4,128)}) custom-call(f32[8,12,128]{2,1,0:T(8,128)} %get-tuple-element.8.by_source, f32[4,32,128]{2,1,0:T(8,128)} %get-tuple-element.9.by_partner, f32[128,1,128]{2,1,0:T(1,128)} %get-tuple-element.10.shares, f32[16,1,128]{2,1,0:T(1,128)} %get-tuple-element.11.parts), custom_call_target="tpu_custom_call" | custom-call | tf_op jit(solution)/shard_map/pallas_call | solution.py:611

commit v8 on v7

--- a/solution.py
+++ b/solution.py
@@ -265,7 +265,7 @@
 
     lax.fori_loop(1, devices, start_meta, 0)
     share = devices // 4
-    for quarter in (2, 1, 3, 0):
+    for quarter in (2, 1, 0, 3):
         lax.fori_loop(quarter * share, (quarter + 1) * share, start_data, 0)
     own_meta = pltpu.make_async_copy(meta.at[me], meta_in.at[me], own.at[1])
     own_meta.start()

time: 38.3 us -> 38.3 us (level)
  no operation moved by 1% of the time
where the time goes in v8:
time: 38.3 us; the launch traced here: 38.1 us
  Pallas kernels  37.4 us (98%)
  between operations  0.64 us (2%)
    pallas_call x1, Pallas kernels, local(): pl.pallas_call(functools.partial(exchange_kernel, cap, n_grp), out_shape=...  35.1 us
    pallas_call x1, Pallas kernels, local(): pl.pallas_call(functools.partial(assemble_kernel, n_grp, width), out_shap...  2.29 us

profile of v8, /device:TPU:9, one launch (start us, length us, event | category | flops | bytes accessed | tf_op | source)
XLA Modules:
  0.0 38.1 jit_solution(4823885283075067943)
XLA Ops:
  0.6 35.1 %shard_map.68 = (f32[8,12,128]{2,1,0:T(8,128)}, f32[4,32,128]{2,1,0:T(8,128)}, f32[128,1,128]{2,1,0:T(1,128)}, f32[16,1,128]{2,1,0:T(1,128)}) custom-call(f32[16,6,16,128]{3,2,1,0:T(8,128)} %bitcast.2, s32[16]{0:T(128)} %count_hbm.1, s32[16,16,128]{2,1,0:T(8,128)} %wanted_hbm.1, s32[16,16]{1,0:T(8,128)} %scans_hbm.1, s32[16,16]{1,0:T(8,128)} %tiles_hbm.1), custom_call_target="tpu_custom_call" | custom-call | tf_op jit(solution)/shard_map/pallas_call | solution.py:573
  35.8 2.3 %shard_map.69 = (f32[6,6,16,32]{3,2,1,0:T(8,128)}, f32[4,6]{1,0:T(4,128)}) custom-call(f32[8,12,128]{2,1,0:T(8,128)} %get-tuple-element.8.by_source, f32[4,32,128]{2,1,0:T(8,128)} %get-tuple-element.9.by_partner, f32[128,1,128]{2,1,0:T(1,128)} %get-tuple-element.10.shares, f32[16,1,128]{2,1,0:T(1,128)} %get-tuple-element.11.parts), custom_call_target="tpu_custom_call" | custom-call | tf_op jit(solution)/shard_map/pallas_call | solution.py:611
